TPU v7x, 128 devices: a whole 4x4x4 slice. The times are simulated.
128 devices in a mesh: dev: 8 (over z_hi, y), ma: 16 (over z_lo, x, core).
Axes of the slice: x: 4, y: 4, z: 4 (z_hi: 2, z_lo: 2; z = z_hi * 2 + z_lo), core: 2. Of those that a mesh axis runs over, the one named last changes fastest.
Arguments:
- joined_weight: bfloat16 [8, 4096, 6144], P(None, 'dev', 'ma'), may hold values from -6 to 6
- norm_gain: float32 [8, 4096], P(None, 'ma'), may hold values from 0.5 to 1.5
- rotary_order: int32 [128], replicated, may hold values from 0 to 127, each once
Outputs:
- query_weight: bfloat16 [8, 4096, 4096], P(None, 'dev', 'ma')
- key_weight: bfloat16 [8, 1024, 4096], P(None, 'dev', 'ma')
- value_weight: bfloat16 [8, 1024, 4096], P(None, 'dev', 'ma')
- row_peak: float32 [8, 6144], P(None, 'dev')
Inputs may be any that keep to these rules, and one draw needn't show every extreme that they name: rotary_order holds every number of 0 to 127 exactly once.
All inputs are finite; a program needn't handle non-finite values.
Results may differ from a plain program's by a relative error of at most 0.0055.
Values may be sent and summed in bfloat16 or wider, within the bound.
No kernel may reach another device: no remote copies, remote signals or barrier semaphores. Data moves between devices by JAX's collectives and lax.ppermute only.
A program may use at most 128 MiB of HBM per device.

v0:
```python
import functools

import jax
import jax.numpy as jnp
import numpy as np
from jax import lax
from jax.experimental import pallas as pl
from jax.experimental.pallas import tpu as pltpu
from jax.sharding import PartitionSpec as P


HEADS = 32
KV_HEADS = 8
GROUP = 4
SLOTS = GROUP + 2
HEAD_TOTAL = HEADS + 2 * KV_HEADS
SIZES = (4, 4)
WHOLE = (False, True)
SIDE = 4
PLACES = 8


def number(a, y, b, x, core):
    return (a * SIDE + y) * 16 + b * 8 + x * 2 + core


def everywhere():
    for n in range(128):
        i, j = divmod(n, 16)
        yield n, i >> 2, i & 3, j >> 3, (j >> 1) & 3, j & 1


def swap(array):
    pairs = [(n, number(a, y, b, x, core ^ 1)) for n, a, y, b, x, core in everywhere()]
    return lax.ppermute(array, ("dev", "ma"), pairs)


def gain_move(gain):
    pairs = [(n, number(b, x, a, y, core)) for n, a, y, b, x, core in everywhere()]
    return lax.ppermute(gain, ("dev", "ma"), pairs)


def first_move(array, r, s):
    pairs = [(n, number(a ^ s, (y + r) % SIDE, b ^ s, x, core)) for n, a, y, b, x, core in everywhere()]
    return lax.ppermute(array, ("dev", "ma"), pairs)


def second_move(array, q, s):
    pairs = [(n, number(a, y, b ^ s, (x + q) % SIDE, core)) for n, a, y, b, x, core in everywhere()]
    return lax.ppermute(array, ("dev", "ma"), pairs)


def position():
    dev = lax.axis_index("dev")
    ma = lax.axis_index("ma")
    return dev >> 2, dev & 3, ma >> 3, (ma >> 1) & 3, ma & 1


def picker(piece):
    columns = piece * HEAD_TOTAL
    pick = np.zeros((columns, columns), np.float32)
    for g in range(KV_HEADS):
        for s in range(SLOTS):
            head = g * GROUP + s if s < GROUP else HEADS + (s - GROUP) * KV_HEADS + g
            for d in range(piece):
                pick[(g * SLOTS + s) * piece + d, d * HEAD_TOTAL + head] = 1.0
    return jnp.asarray(pick, jnp.bfloat16)


def prepare_body(first, place_ref, pick_ref, gain_ref, own_ref, other_ref, *refs):
    out_refs = refs[:-1]
    turned_ref = refs[-1]
    width = own_ref.shape[1]
    contract = (((1,), (1,)), ((), ()))

    def turned(ref):
        rows = lax.dot_general(pick_ref[...], ref[0], contract, preferred_element_type=jnp.float32)
        return rows.reshape(KV_HEADS * SLOTS, -1, width)

    both = jnp.concatenate([turned(own_ref), turned(other_ref)], axis=1)
    both = both.reshape(-1, width)
    if len(out_refs) == 1:
        both = both * gain_ref[pl.ds(first + pl.program_id(0), 1), :]
    turned_ref[...] = both.astype(jnp.bfloat16)
    rows = turned_ref.shape[0] // KV_HEADS
    if len(out_refs) == 1:
        out_refs[0][:, 0] = turned_ref[...].reshape(KV_HEADS, rows, width)
        return
    a = place_ref[1]
    y = place_ref[2]
    for s in range(2):
        for r in range(SIDE):
            g = (a ^ s) * SIDE + ((y + r) & (SIDE - 1))
            out_refs[s * SIDE + r][0] = turned_ref[pl.ds(pl.multiple_of(g * rows, 16), rows), :]


def prepare(stored, other, gain, place, first, whole):
    _, features, columns = stored.shape
    layers = other.shape[0]
    width = features // 2
    rows = 2 * columns // KV_HEADS
    if whole:
        out_specs = [pl.BlockSpec((PLACES, 1, rows, width), lambda l, place: (0, l, 0, 0))]
        out_shape = [jax.ShapeDtypeStruct((PLACES, layers, rows, width), jnp.bfloat16)]
    else:
        out_specs = [pl.BlockSpec((1, rows, width), lambda l, place: (l, 0, 0))] * PLACES
        out_shape = [jax.ShapeDtypeStruct((layers, rows, width), jnp.bfloat16)] * PLACES
    return pl.pallas_call(
        functools.partial(prepare_body, first),
        grid_spec=pltpu.PrefetchScalarGridSpec(
            num_scalar_prefetch=1,
            grid=(layers,),
            in_specs=[
                pl.BlockSpec((columns, columns), lambda l, place: (0, 0)),
                pl.BlockSpec(gain.shape, lambda l, place: (0, 0)),
                pl.BlockSpec((1, width, columns), lambda l, place: (first + l, place[0], 0)),
                pl.BlockSpec((1, width, columns), lambda l, place: (l, 0, 0)),
            ],
            out_specs=out_specs,
            scratch_shapes=[pltpu.VMEM((2 * columns, width), jnp.bfloat16)],
        ),
        out_shape=out_shape,
        name="prepare",
    )(place, picker(columns // HEAD_TOTAL), gain, stored, other)


def reorder_body(*refs):
    in_refs = refs[:PLACES]
    out_refs = refs[PLACES : 2 * PLACES]
    held_ref, in_sems, out_sems = refs[2 * PLACES :]
    a, y, b, x, _ = position()
    flip = a ^ b
    turn = (y - x) & (SIDE - 1)
    for f in range(2):
        for t in range(SIDE):

            @pl.when((flip == f) & (turn == t))
            def _(f=f, t=t):
                for s in range(2):
                    for q in range(SIDE):
                        source = (s ^ f) * SIDE + ((t - q) & (SIDE - 1))
                        k = s * SIDE + q
                        pltpu.make_async_copy(in_refs[source], held_ref.at[k], in_sems.at[k]).start()

    for k in range(PLACES):
        pltpu.make_async_copy(in_refs[k], held_ref.at[k], in_sems.at[k]).wait()
        pltpu.make_async_copy(held_ref.at[k], out_refs[k], out_sems.at[k]).start()
    for k in range(PLACES):
        pltpu.make_async_copy(held_ref.at[k], out_refs[k], out_sems.at[k]).wait()


def reorder(buffers):
    spec = pl.BlockSpec(memory_space=pltpu.HBM)
    shape = buffers[0].shape
    return pl.pallas_call(
        reorder_body,
        in_specs=[spec] * PLACES,
        out_specs=[spec] * PLACES,
        out_shape=[jax.ShapeDtypeStruct(shape, v.dtype) for v in buffers],
        scratch_shapes=[
            pltpu.VMEM((PLACES, *shape), jnp.bfloat16),
            pltpu.SemaphoreType.DMA((PLACES,)),
            pltpu.SemaphoreType.DMA((PLACES,)),
        ],
        name="reorder",
    )(*buffers)


def peak_body(*refs):
    moved_refs, out_ref = refs[:-1], refs[-1]
    _, _, width = moved_refs[0].shape
    for u in range(2):
        size = jnp.abs(moved_refs[u * SIDE][...])
        for v in range(1, SIDE):
            size = jnp.maximum(size, jnp.abs(moved_refs[u * SIDE + v][...]))
        size = size.reshape(-1, width).astype(jnp.float32)
        size = jnp.maximum(size[:, :128], size[:, 128:])
        out_ref[u : u + 1, :] = jnp.max(size.T, axis=0, keepdims=True)


def peaks(moved):
    layers, rows, width = moved[0].shape[-3:]
    if len(moved) == 1:
        held = [
            pl.BlockSpec((None, layers, rows, width), lambda l, k=k: (k, 0, 0, 0)) for k in range(PLACES)
        ]
        moved = moved * PLACES
    else:
        held = [pl.BlockSpec((layers, rows, width), lambda l: (0, 0, 0))] * PLACES
    return pl.pallas_call(
        peak_body,
        grid=(1,),
        in_specs=held,
        out_specs=pl.BlockSpec((2, layers * rows), lambda l: (0, 0)),
        out_shape=jax.ShapeDtypeStruct((2, layers * rows), jnp.float32),
        name="peaks",
    )(*moved)


def placed_peaks(found, whole):
    a, _, b, x, core = position()
    found = found.reshape(2, -1, SLOTS, 2, PLACES)
    found = jnp.where(core == 1, found[:, :, :, ::-1], found)
    u = jnp.arange(2)[:, None]
    upper = u ^ a ^ b if whole else u ^ a
    here = jnp.arange(PLACES)[None, :] == upper * SIDE + x
    spread = jnp.where(here[:, None, None, :, None, None], found[:, :, :, None], 0.0)
    return spread.max(0).reshape(found.shape[1], -1).astype(jnp.bfloat16)


def finish_body(turn_ref, gain_ref, first, *refs):
    moved_refs = refs[:PLACES]
    outs = refs[PLACES:]
    if gain_ref is None:
        query_ref, key_ref, value_ref = outs[-3:]
    else:
        query_ref, key_ref, value_ref, peak_ref = outs[-4:]
    _, rows, _ = moved_refs[0].shape
    piece = rows // SLOTS
    dim = PLACES * piece
    for s in range(SLOTS):
        held = jnp.concatenate([ref[0, s * piece : (s + 1) * piece, :] for ref in moved_refs], axis=0)
        turned = jnp.dot(turn_ref[s // (SLOTS - 1)], held, preferred_element_type=jnp.float32)
        if gain_ref is not None:
            turned = turned * gain_ref[pl.ds(first + pl.program_id(0), 1), :]
        turned = turned.astype(jnp.bfloat16)
        if s < GROUP:
            query_ref[0, s * dim : (s + 1) * dim, :] = turned
        elif s == GROUP:
            key_ref[0] = turned
        else:
            value_ref[0] = turned
        if gain_ref is not None:
            size = jnp.abs(turned.astype(jnp.float32))
            size = jnp.maximum(size[:, :128], size[:, 128:])
            peak_ref[0, :, s * dim : (s + 1) * dim] = jnp.max(size.T, axis=0, keepdims=True)


def plain_body(turn_ref, *refs):
    finish_body(turn_ref, None, 0, *refs)


def scaled_body(first, turn_ref, gain_ref, *refs):
    finish_body(turn_ref, gain_ref, first, *refs)


def finish(moved, turn, gain, whole, first, earlier):
    layers, rows, width = moved[0].shape[-3:]
    dim = turn.shape[1]

    def at(*shape):
        return pl.BlockSpec((1, *shape), lambda l: (first + l, 0, 0))

    shapes = [
        ((GROUP * dim, width), jnp.bfloat16),
        ((dim, width), jnp.bfloat16),
        ((dim, width), jnp.bfloat16),
    ]
    out_specs = [at(*shape) for shape, _ in shapes]
    out_shape = [jax.ShapeDtypeStruct((whole, *shape), kind) for shape, kind in shapes]
    before = [turn]
    in_specs = [pl.BlockSpec((2, dim, dim), lambda l: (0, 0, 0))]
    body = plain_body
    if gain is not None:
        body = functools.partial(scaled_body, first)
        before.append(gain)
        in_specs.append(pl.BlockSpec(gain.shape, lambda l: (0, 0)))
        out_specs.append(pl.BlockSpec((1, 1, SLOTS * dim), lambda l: (l, 0, 0)))
        out_shape.append(jax.ShapeDtypeStruct((layers, 1, SLOTS * dim), jnp.float32))
    if len(moved) == 1:
        held = [
            pl.BlockSpec((None, 1, rows, width), lambda l, k=k: (k, l, 0, 0)) for k in range(PLACES)
        ]
        moved = moved * PLACES
    else:
        held = [pl.BlockSpec((1, rows, width), lambda l: (l, 0, 0))] * PLACES
    shapes = [
        ((GROUP * dim, width), jnp.bfloat16),
        ((dim, width), jnp.bfloat16),
        ((dim, width), jnp.bfloat16),
    ]
    return pl.pallas_call(
        body,
        grid=(layers,),
        in_specs=in_specs + held + [pl.BlockSpec(memory_space=pltpu.HBM)] * len(earlier),
        out_specs=out_specs,
        out_shape=out_shape,
        input_output_aliases={len(before) + PLACES + k: k for k in range(len(earlier))},
        name="finish",
    )(*before, *moved, *earlier)


def turning(rotary_order, whole):
    dim = rotary_order.shape[0]
    piece = dim // PLACES
    a, _, b, x, core = position()
    place = jnp.arange(dim, dtype=jnp.int32)
    u = place // (SIDE * piece)
    v = (place // piece) & (SIDE - 1)
    t = place & (piece - 1)
    high, low = (u ^ a ^ b, v) if whole else (u ^ a, (x - v) & (SIDE - 1))
    holds = (high * SIDE + low) * piece + (t ^ (core * (piece // 2)))
    orders = jnp.stack([rotary_order, place])
    return (orders[:, :, None] == holds[None, None, :]).astype(jnp.bfloat16)


FIRST_GROUPS = [
    [number(a, y, a ^ key, x, core) for a in range(2) for y in range(SIDE)]
    for key in range(2)
    for x in range(SIDE)
    for core in range(2)
]
SECOND_GROUPS = [
    [number(a, y, b, x, core) for b in range(2) for x in range(SIDE)]
    for a in range(2)
    for y in range(SIDE)
    for core in range(2)
]


def exchange(array, groups):
    return lax.all_to_all(array, ("dev", "ma"), 0, 0, tiled=True, axis_index_groups=groups)


STAGE = ((1, 0), (3, 0), (2, 0), (0, 1), (1, 1), (3, 1), (2, 1))


def staged(buffers, move):
    out = list(buffers)
    for step, s in STAGE:
        k = s * SIDE + step
        out[k] = move(buffers[k], step, s)
    return out


def shards(joined_weight, norm_gain, rotary_order):
    layers, features, columns = joined_weight.shape
    width = features // 2
    dim = rotary_order.shape[0]
    a, y, _, _, core = position()
    place = jnp.stack([core, a, y]).astype(jnp.int32)
    turns = [turning(rotary_order, False), turning(rotary_order, True)]
    firsts = [sum(SIZES[:k]) for k in range(len(SIZES))]
    gain = gain_move(norm_gain)
    moved = []
    for first, size, whole in zip(firsts, SIZES, WHOLE):
        theirs = lax.dynamic_slice(
            joined_weight, (first, (1 - core) * width, 0), (size, width, columns)
        )
        theirs = swap(theirs)
        blocks = prepare(joined_weight, theirs, gain if whole else norm_gain, place, first, whole)
        moved.append([exchange(blocks[0], FIRST_GROUPS)] if whole else staged(blocks, first_move))
    outs = []
    found = []
    for first, buffers, whole in zip(firsts, moved, WHOLE):
        if not whole:
            buffers = reorder(buffers)
        else:
            found.append(placed_peaks(peaks(buffers), whole))
        if whole:
            arrived = [exchange(buffers[0], SECOND_GROUPS)]
        else:
            arrived = staged(buffers, second_move)
        own = None if whole else norm_gain
        outs = list(finish(arrived, turns[whole], own, layers, first, outs))
        if not whole:
            found.append(outs.pop()[:, 0].astype(jnp.bfloat16))
    peak = jnp.concatenate(found, axis=0)
    for steps in JOINS:
        others = [lax.ppermute(peak, "ma", [(j, j ^ step) for j in range(16)]) for step in steps]
        for other in others:
            peak = jnp.maximum(peak, other)
    ready, stored = peak[: SIZES[0]], peak[SIZES[0] :].reshape(-1, SLOTS, dim)
    orders = (rotary_order[None, :] == jnp.arange(dim, dtype=jnp.int32)[:, None]).astype(jnp.bfloat16)
    turned = jnp.dot(stored[:, :-1].reshape(-1, dim), orders, preferred_element_type=jnp.float32)
    turned = turned.reshape(-1, SLOTS - 1, dim)
    turned = jnp.concatenate([turned, stored[:, -1:].astype(jnp.float32)], axis=1)
    row_peak = jnp.concatenate([ready.astype(jnp.float32), turned.reshape(-1, SLOTS * dim)], axis=0)
    query, key, value = outs
    return query, key, value, row_peak


JOINS = ((1,), (8,), (2, 4, 6))


def solution(mesh):
    return jax.shard_map(
        shards,
        mesh=mesh,
        in_specs=(P(None, "dev", "ma"), P(None, "ma"), P()),
        out_specs=(
            P(None, "dev", "ma"),
            P(None, "dev", "ma"),
            P(None, "dev", "ma"),
            P(None, "dev"),
        ),
        check_vma=False,
    )
```

profile of v0, /device:TPU:2, one launch (start us, length us, event | category | flops | bytes accessed | tf_op | source)
XLA Modules:
  0.0 142.2 jit_solution(1091205137891100144)
XLA Ops:
  0.7 1.6 %constant_dynamic-slice_fusion = (bf16[4,256,384]{2,1,0:T(8,128)(2,1)S(1)}, bf16[4,256,384]{2,1,0:T(8,128)(2,1)S(1)}) fusion(bf16[8,512,384]{2,1,0:T(8,128)(2,1)} %own_ref.3, s32[]{:T(128)S(6)} %select_n.44), kind=kLoop, calls=%fused_computation.33 | loop fusion | bytes 3145732 | tf_op jit(solution)/shard_map/dynamic_slice | solution.py:347
  2.8 3.4 %collective-permute-start = (f32[8,256]{1,0:T(8,128)S(1)}, f32[8,256]{1,0:T(8,128)S(1)}, u32[]{:S(2)}, u32[]{:S(2)}) collective-permute-start(f32[8,256]{1,0:T(8,128)S(1)} %copy-done.18), channel_id=1, source_target_pairs={{0,0},{1,1},{2,16},{3,17},{4,32},{5,33},{6,48},{7,49},{8,64},{9,65... | collective-permute-start | bytes 24584 | tf_op jit(solution)/shard_map/ppermute | solution.py:40
  6.9 2.4 %collective-permute-done.gain_ref = f32[8,256]{1,0:T(8,128)S(1)} collective-permute-done((f32[8,256]{1,0:T(8,128)S(1)}, f32[8,256]{1,0:T(8,128)S(1)}, u32[]{:S(2)}, u32[]{:S(2)}) %collective-permute-start) | collective-permute-done | bytes 8224 | tf_op jit(solution)/shard_map/ppermute | solution.py:40
  10.7 5.3 %prepare.2 = bf16[8,4,96,256]{3,2,1,0:T(8,128)(2,1)} custom-call(s32[3]{0:T(128)} %pad_add_fusion.1.place_ref, bf16[384,384]{1,0:T(8,128)(2,1)} %constant.73.clone.pick_ref, f32[8,256]{1,0:T(8,128)} %copy-done.19, bf16[8,512,384]{2,1,0:T(8,128)(2,1)} %own_ref.3, bf16[4,256,384]{2,1,0:T(8,128)(2,1)} %copy-done.3), custom_call_target="tpu_custom_call" | custom-call | tf_op jit(solution)/shard_map/prepare/pallas_call | solution.py:108
  16.0 10.8 %all-to-all-start = ((bf16[8,4,96,256]{3,2,1,0:T(8,128)(2,1)}), bf16[8,4,96,256]{3,2,1,0:T(8,128)(2,1)S(1)}, u32[]{:S(2)}, u32[]{:S(2)}) async-start(bf16[8,4,96,256]{3,2,1,0:T(8,128)(2,1)} %prepare.2), calls=%async_computation | async-start | bytes 3145728 | tf_op jit(solution)/shard_map/all_to_all | solution.py:322
  27.7 5.2 %prepare.3 = (bf16[4,96,256]{2,1,0:T(8,128)(2,1)}, bf16[4,96,256]{2,1,0:T(8,128)(2,1)}, bf16[4,96,256]{2,1,0:T(8,128)(2,1)}, bf16[4,96,256]{2,1,0:T(8,128)(2,1)}...) custom-call(s32[3]{0:T(128)} %pad_add_fusion.1.place_ref, ...), custom_call_target="tpu_custom_call" | custom-call | tf_op jit(solution)/shard_map/prepare/pallas_call | solution.py:108
  32.8 2.1 %collective-permute-start.3 = (bf16[4,96,256]{2,1,0:T(8,128)(2,1)}, bf16[4,96,256]{2,1,0:T(8,128)(2,1)S(1)}, u32[]{:S(2)}, u32[]{:S(2)}) collective-permute-start(bf16[4,96,256]{2,1,0:T(8,128)(2,1)} %get-tuple-element.28), channel_id=1, source_target_pairs={{0,16},{1,17},{2,18},{3,19},{4,20},{5,21},{6,22},{7,23},{8,24},{9,... | collective-permute-start | bytes 589832 | tf_op jit(solution)/shard_map/ppermute | solution.py:45
  34.9 2.7 %collective-permute-start.4 = (bf16[4,96,256]{2,1,0:T(8,128)(2,1)}, bf16[4,96,256]{2,1,0:T(8,128)(2,1)S(1)}, u32[]{:S(2)}, u32[]{:S(2)}) collective-permute-start(bf16[4,96,256]{2,1,0:T(8,128)(2,1)} %get-tuple-element.29), channel_id=1, source_target_pairs={{0,32},{1,33},{2,34},{3,35},{4,36},{5,37},{6,38},{7,39},{8,40},{9,... | collective-permute-start | bytes 589832 | tf_op jit(solution)/shard_map/ppermute | solution.py:45
  37.6 1.5 %collective-permute-start.5 = (bf16[4,96,256]{2,1,0:T(8,128)(2,1)}, bf16[4,96,256]{2,1,0:T(8,128)(2,1)S(1)}, u32[]{:S(2)}, u32[]{:S(2)}) collective-permute-start(bf16[4,96,256]{2,1,0:T(8,128)(2,1)} %get-tuple-element.30), channel_id=1, source_target_pairs={{0,48},{1,49},{2,50},{3,51},{4,52},{5,53},{6,54},{7,55},{8,56},{9,... | collective-permute-start | bytes 589832 | tf_op jit(solution)/shard_map/ppermute | solution.py:45
  39.1 2.7 %collective-permute-start.6 = (bf16[4,96,256]{2,1,0:T(8,128)(2,1)}, bf16[4,96,256]{2,1,0:T(8,128)(2,1)S(1)}, u32[]{:S(2)}, u32[]{:S(2)}) collective-permute-start(bf16[4,96,256]{2,1,0:T(8,128)(2,1)} %get-tuple-element.31), channel_id=1, source_target_pairs={{0,72},{1,73},{2,74},{3,75},{4,76},{5,77},{6,78},{7,79},{8,64},{9,... | collective-permute-start | bytes 589832 | tf_op jit(solution)/shard_map/ppermute | solution.py:45
  42.4 10.7 %collective-permute-done.3.refs_1_ = bf16[4,96,256]{2,1,0:T(8,128)(2,1)S(1)} collective-permute-done((bf16[4,96,256]{2,1,0:T(8,128)(2,1)}, bf16[4,96,256]{2,1,0:T(8,128)(2,1)S(1)}, u32[]{:S(2)}, u32[]{:S(2)}) %collective-permute-start.3) | collective-permute-done | bytes 196640 | tf_op jit(solution)/shard_map/ppermute | solution.py:45
  53.1 3.1 %collective-permute-start.8 = (bf16[4,96,256]{2,1,0:T(8,128)(2,1)}, bf16[4,96,256]{2,1,0:T(8,128)(2,1)S(1)}, u32[]{:S(2)}, u32[]{:S(2)}) collective-permute-start(bf16[4,96,256]{2,1,0:T(8,128)(2,1)} %get-tuple-element.33), channel_id=1, source_target_pairs={{0,104},{1,105},{2,106},{3,107},{4,108},{5,109},{6,110},{7,111},{8... | collective-permute-start | bytes 589832 | tf_op jit(solution)/shard_map/ppermute | solution.py:45
  56.1 1.1 collective-permute-done.4.refs_2_
  57.4 11.3 %collective-permute-done.7.refs_5_ = bf16[4,96,256]{2,1,0:T(8,128)(2,1)S(1)} collective-permute-done((bf16[4,96,256]{2,1,0:T(8,128)(2,1)}, bf16[4,96,256]{2,1,0:T(8,128)(2,1)S(1)}, u32[]{:S(2)}, u32[]{:S(2)}) %collective-permute-start.7) | collective-permute-done | bytes 196640 | tf_op jit(solution)/shard_map/ppermute | solution.py:45
  70.2 2.3 %reorder.1 = (bf16[4,96,256]{2,1,0:T(8,128)(2,1)}, bf16[4,96,256]{2,1,0:T(8,128)(2,1)}, bf16[4,96,256]{2,1,0:T(8,128)(2,1)}, bf16[4,96,256]{2,1,0:T(8,128)(2,1)}...) custom-call(bf16[4,96,256]{2,1,0:T(8,128)(2,1)} %get-tuple-element.2, ...), custom_call_target="tpu_custom_call" | custom-call | tf_op jit(solution)/shard_map/reorder/pallas_call | solution.py:155
  72.6 2.8 %collective-permute-start.11 = (bf16[4,96,256]{2,1,0:T(8,128)(2,1)}, bf16[4,96,256]{2,1,0:T(8,128)(2,1)S(1)}, u32[]{:S(2)}, u32[]{:S(2)}) collective-permute-start(bf16[4,96,256]{2,1,0:T(8,128)(2,1)} %get-tuple-element.37), channel_id=1, source_target_pairs={{0,4},{1,5},{2,6},{3,7},{4,0},{5,1},{6,2},{7,3},{8,12},{9,13},{10,... | collective-permute-start | bytes 589832 | tf_op jit(solution)/shard_map/ppermute | solution.py:50
  76.7 3.0 %collective-permute-start.14 = (bf16[4,96,256]{2,1,0:T(8,128)(2,1)}, bf16[4,96,256]{2,1,0:T(8,128)(2,1)S(1)}, u32[]{:S(2)}, u32[]{:S(2)}) collective-permute-start(bf16[4,96,256]{2,1,0:T(8,128)(2,1)} %get-tuple-element.40), channel_id=1, source_target_pairs={{0,10},{1,11},{2,12},{3,13},{4,14},{5,15},{6,8},{7,9},{8,2},{9,3},... | collective-permute-start | bytes 589832 | tf_op jit(solution)/shard_map/ppermute | solution.py:50
  79.6 0.9 collective-permute-done.10.refs_1_
  81.4 3.3 %collective-permute-start.16 = (bf16[4,96,256]{2,1,0:T(8,128)(2,1)}, bf16[4,96,256]{2,1,0:T(8,128)(2,1)S(1)}, u32[]{:S(2)}, u32[]{:S(2)}) collective-permute-start(bf16[4,96,256]{2,1,0:T(8,128)(2,1)} %get-tuple-element.42), channel_id=1, source_target_pairs={{0,14},{1,15},{2,8},{3,9},{4,10},{5,11},{6,12},{7,13},{8,6},{9,7},... | collective-permute-start | bytes 589832 | tf_op jit(solution)/shard_map/ppermute | solution.py:50
  84.7 2.4 %collective-permute-done.12.refs_3_ = bf16[4,96,256]{2,1,0:T(8,128)(2,1)S(1)} collective-permute-done((bf16[4,96,256]{2,1,0:T(8,128)(2,1)}, bf16[4,96,256]{2,1,0:T(8,128)(2,1)S(1)}, u32[]{:S(2)}, u32[]{:S(2)}) %collective-permute-start.12) | collective-permute-done | bytes 196640 | tf_op jit(solution)/shard_map/ppermute | solution.py:50
  87.1 5.8 %collective-permute-done.13.refs_4_ = bf16[4,96,256]{2,1,0:T(8,128)(2,1)S(1)} collective-permute-done((bf16[4,96,256]{2,1,0:T(8,128)(2,1)}, bf16[4,96,256]{2,1,0:T(8,128)(2,1)S(1)}, u32[]{:S(2)}, u32[]{:S(2)}) %collective-permute-start.13) | collective-permute-done | bytes 196640 | tf_op jit(solution)/shard_map/ppermute | solution.py:50
  93.9 4.1 %finish.2 = (bf16[8,512,256]{2,1,0:T(8,128)(2,1)}, bf16[8,128,256]{2,1,0:T(8,128)(2,1)}, bf16[8,128,256]{2,1,0:T(8,128)(2,1)}, f32[4,1,768]{2,1,0:T(1,128)}) custom-call(bf16[2,128,128]{2,1,0:T(8,128)(2,1)} %get-tuple-element.54.turn_ref, f32[8,256]{1,0:T(8,128)} %gain_ref.3, bf16[4,96,256]{2,1,0:T(8,128)(2,1)} %get-tuple-element.35.refs_0_, ...), custom_call_target="tpu_custom_call" | custom-call | tf_op jit(solution)/shard_map/finish/pallas_call | solution.py:282
  98.7 1.2 copy-done
  99.9 2.3 %peaks.1 = f32[2,384]{1,0:T(2,128)} custom-call(bf16[8,4,96,256]{3,2,1,0:T(8,128)(2,1)} %copy-done, bf16[8,4,96,256]{3,2,1,0:T(8,128)(2,1)} %copy-done, bf16[8,4,96,256]{3,2,1,0:T(8,128)(2,1)} %copy-done, bf16[8,4,96,256]{3,2,1,0:T(8,128)(2,1)} %copy-done, bf16[8,4,96,256]{3,2,1,0:T(8,128)(2,1)} %copy-done, bf16[8,4,96,256]{3,2,1,0:T(8,128)(2,1)} %copy-done, ...), custom_call_target="tpu_custom_call" | custom-call | tf_op jit(solution)/shard_map/peaks/pallas_call | solution.py:190
  103.6 6.0 %all-to-all-start.1 = ((bf16[8,4,96,256]{3,2,1,0:T(8,128)(2,1)}), bf16[8,4,96,256]{3,2,1,0:T(8,128)(2,1)S(1)}, u32[]{:S(2)}, u32[]{:S(2)}) async-start(bf16[8,4,96,256]{3,2,1,0:T(8,128)(2,1)} %copy-done), calls=%async_computation.1 | async-start | bytes 3145728 | tf_op jit(solution)/shard_map/all_to_all | solution.py:322
  109.6 1.6 %collective-permute-start.18 = (bf16[8,768]{1,0:T(8,128)(2,1)S(1)}, bf16[8,768]{1,0:T(8,128)(2,1)S(1)}, u32[]{:S(2)}, u32[]{:S(2)}) collective-permute-start(bf16[8,768]{1,0:T(8,128)(2,1)S(1)} %fusion.8), channel_id=1, source_target_pairs={{0,8},{1,9},{2,10},{3,11},{4,12},{5,13},{6,14},{7,15},{8,0},{9,1},... | collective-permute-start | bytes 36872 | tf_op jit(solution)/shard_map/ppermute | solution.py:370
  111.2 5.6 %collective-permute-done.18 = bf16[8,768]{1,0:T(8,128)(2,1)S(1)} collective-permute-done((bf16[8,768]{1,0:T(8,128)(2,1)S(1)}, bf16[8,768]{1,0:T(8,128)(2,1)S(1)}, u32[]{:S(2)}, u32[]{:S(2)}) %collective-permute-start.18) | collective-permute-done | bytes 12320 | tf_op jit(solution)/shard_map/ppermute | solution.py:370
  116.8 14.1 %collective-permute-start.21 = (bf16[8,768]{1,0:T(8,128)(2,1)S(1)}, bf16[8,768]{1,0:T(8,128)(2,1)S(1)}, u32[]{:S(2)}, u32[]{:S(2)}) collective-permute-start(bf16[8,768]{1,0:T(8,128)(2,1)S(1)} %max.16), channel_id=1, source_target_pairs={{0,6},{1,7},{2,4},{3,5},{4,2},{5,3},{6,0},{7,1},{8,14},{9,15},{10,... | collective-permute-start | bytes 36872 | tf_op jit(solution)/shard_map/ppermute | solution.py:370
  130.9 2.2 %collective-permute-start.19 = (bf16[8,768]{1,0:T(8,128)(2,1)S(1)}, bf16[8,768]{1,0:T(8,128)(2,1)S(1)}, u32[]{:S(2)}, u32[]{:S(2)}) collective-permute-start(bf16[8,768]{1,0:T(8,128)(2,1)S(1)} %max.16), channel_id=1, source_target_pairs={{0,2},{1,3},{2,0},{3,1},{4,6},{5,7},{6,4},{7,5},{8,10},{9,11},{10,... | collective-permute-start | bytes 36872 | tf_op jit(solution)/shard_map/ppermute | solution.py:370
  133.1 3.0 %collective-permute-done.20 = bf16[8,768]{1,0:T(8,128)(2,1)S(1)} collective-permute-done((bf16[8,768]{1,0:T(8,128)(2,1)S(1)}, bf16[8,768]{1,0:T(8,128)(2,1)S(1)}, u32[]{:S(2)}, u32[]{:S(2)}) %collective-permute-start.20) | collective-permute-done | bytes 12320 | tf_op jit(solution)/shard_map/ppermute | solution.py:370
  137.0 1.2 copy-done.1
  138.2 4.0 %finish.3 = (bf16[8,512,256]{2,1,0:T(8,128)(2,1)}, bf16[8,128,256]{2,1,0:T(8,128)(2,1)}, bf16[8,128,256]{2,1,0:T(8,128)(2,1)}) custom-call(bf16[2,128,128]{2,1,0:T(8,128)(2,1)} %get-tuple-element.55.turn_ref, bf16[8,4,96,256]{3,2,1,0:T(8,128)(2,1)} %copy-done.1, ...), custom_call_target="tpu_custom_call", output_to_operand_aliasing={{0}: (9, {}), {1}: (10, {}), {2}: (11, {})} | custom-call | tf_op jit(solution)/shard_map/finish/pallas_call | solution.py:282
  (92 shorter events, 11.7 us)
Async XLA Ops:
  2.2 7.0 %collective-permute-start.1 = (bf16[4,256,384]{2,1,0:T(8,128)(2,1)S(1)}, bf16[4,256,384]{2,1,0:T(8,128)(2,1)S(1)}, u32[]{:S(2)}, u32[]{:S(2)}) collective-permute-start(bf16[4,256,384]{2,1,0:T(8,128)(2,1)S(1)} %get-tuple-element.51), channel_id=1, source_target_pairs={{0,1},{1,0},{2,3},{3,2},{4,5},{5,4},{6,7},{7,6},{8,9},{9,8},{10,11... | collective-permute-start | bytes 2359304 | tf_op jit(solution)/shard_map/ppermute | solution.py:35
  2.3 24.5 %collective-permute-start.2 = (bf16[4,256,384]{2,1,0:T(8,128)(2,1)S(1)}, bf16[4,256,384]{2,1,0:T(8,128)(2,1)S(1)}, u32[]{:S(2)}, u32[]{:S(2)}) collective-permute-start(bf16[4,256,384]{2,1,0:T(8,128)(2,1)S(1)} %get-tuple-element.50), channel_id=1, source_target_pairs={{0,1},{1,0},{2,3},{3,2},{4,5},{5,4},{6,7},{7,6},{8,9},{9,8},{10,11... | collective-permute-start | bytes 2359304 | tf_op jit(solution)/shard_map/ppermute | solution.py:35
  2.8 6.4 %collective-permute-start = (f32[8,256]{1,0:T(8,128)S(1)}, f32[8,256]{1,0:T(8,128)S(1)}, u32[]{:S(2)}, u32[]{:S(2)}) collective-permute-start(f32[8,256]{1,0:T(8,128)S(1)} %copy-done.18), channel_id=1, source_target_pairs={{0,0},{1,1},{2,16},{3,17},{4,32},{5,33},{6,48},{7,49},{8,64},{9,65... | collective-permute-start | bytes 24584 | tf_op jit(solution)/shard_map/ppermute | solution.py:40
  16.0 82.7 %all-to-all-start = ((bf16[8,4,96,256]{3,2,1,0:T(8,128)(2,1)}), bf16[8,4,96,256]{3,2,1,0:T(8,128)(2,1)S(1)}, u32[]{:S(2)}, u32[]{:S(2)}) async-start(bf16[8,4,96,256]{3,2,1,0:T(8,128)(2,1)} %prepare.2), calls=%async_computation | async-start | bytes 3145728 | tf_op jit(solution)/shard_map/all_to_all | solution.py:322
  26.8 30.5 %copy-start.20 = (s32[128]{0:T(128)S(1)}, s32[128]{0:T(128)}, u32[]{:S(2)}) copy-start(s32[128]{0:T(128)} %param.7) | copy-start | bytes 1540
  32.8 20.2 %collective-permute-start.3 = (bf16[4,96,256]{2,1,0:T(8,128)(2,1)}, bf16[4,96,256]{2,1,0:T(8,128)(2,1)S(1)}, u32[]{:S(2)}, u32[]{:S(2)}) collective-permute-start(bf16[4,96,256]{2,1,0:T(8,128)(2,1)} %get-tuple-element.28), channel_id=1, source_target_pairs={{0,16},{1,17},{2,18},{3,19},{4,20},{5,21},{6,22},{7,23},{8,24},{9,... | collective-permute-start | bytes 589832 | tf_op jit(solution)/shard_map/ppermute | solution.py:45
  34.9 22.3 %collective-permute-start.4 = (bf16[4,96,256]{2,1,0:T(8,128)(2,1)}, bf16[4,96,256]{2,1,0:T(8,128)(2,1)S(1)}, u32[]{:S(2)}, u32[]{:S(2)}) collective-permute-start(bf16[4,96,256]{2,1,0:T(8,128)(2,1)} %get-tuple-element.29), channel_id=1, source_target_pairs={{0,32},{1,33},{2,34},{3,35},{4,36},{5,37},{6,38},{7,39},{8,40},{9,... | collective-permute-start | bytes 589832 | tf_op jit(solution)/shard_map/ppermute | solution.py:45
  37.6 19.7 %collective-permute-start.5 = (bf16[4,96,256]{2,1,0:T(8,128)(2,1)}, bf16[4,96,256]{2,1,0:T(8,128)(2,1)S(1)}, u32[]{:S(2)}, u32[]{:S(2)}) collective-permute-start(bf16[4,96,256]{2,1,0:T(8,128)(2,1)} %get-tuple-element.30), channel_id=1, source_target_pairs={{0,48},{1,49},{2,50},{3,51},{4,52},{5,53},{6,54},{7,55},{8,56},{9,... | collective-permute-start | bytes 589832 | tf_op jit(solution)/shard_map/ppermute | solution.py:45
  39.1 18.2 %collective-permute-start.6 = (bf16[4,96,256]{2,1,0:T(8,128)(2,1)}, bf16[4,96,256]{2,1,0:T(8,128)(2,1)S(1)}, u32[]{:S(2)}, u32[]{:S(2)}) collective-permute-start(bf16[4,96,256]{2,1,0:T(8,128)(2,1)} %get-tuple-element.31), channel_id=1, source_target_pairs={{0,72},{1,73},{2,74},{3,75},{4,76},{5,77},{6,78},{7,79},{8,64},{9,... | collective-permute-start | bytes 589832 | tf_op jit(solution)/shard_map/ppermute | solution.py:45
  41.8 26.8 %collective-permute-start.7 = (bf16[4,96,256]{2,1,0:T(8,128)(2,1)}, bf16[4,96,256]{2,1,0:T(8,128)(2,1)S(1)}, u32[]{:S(2)}, u32[]{:S(2)}) collective-permute-start(bf16[4,96,256]{2,1,0:T(8,128)(2,1)} %get-tuple-element.32), channel_id=1, source_target_pairs={{0,88},{1,89},{2,90},{3,91},{4,92},{5,93},{6,94},{7,95},{8,80},{9,... | collective-permute-start | bytes 589832 | tf_op jit(solution)/shard_map/ppermute | solution.py:45
  53.1 16.5 %copy-start.4 = (bf16[4,96,256]{2,1,0:T(8,128)(2,1)}, bf16[4,96,256]{2,1,0:T(8,128)(2,1)S(1)}, u32[]{:S(2)}) copy-start(bf16[4,96,256]{2,1,0:T(8,128)(2,1)S(1)} %collective-permute-done.3.refs_1_) | copy-start | bytes 589828
  53.1 15.6 %collective-permute-start.8 = (bf16[4,96,256]{2,1,0:T(8,128)(2,1)}, bf16[4,96,256]{2,1,0:T(8,128)(2,1)S(1)}, u32[]{:S(2)}, u32[]{:S(2)}) collective-permute-start(bf16[4,96,256]{2,1,0:T(8,128)(2,1)} %get-tuple-element.33), channel_id=1, source_target_pairs={{0,104},{1,105},{2,106},{3,107},{4,108},{5,109},{6,110},{7,111},{8... | collective-permute-start | bytes 589832 | tf_op jit(solution)/shard_map/ppermute | solution.py:45
  57.3 12.3 %copy-start.5 = (bf16[4,96,256]{2,1,0:T(8,128)(2,1)}, bf16[4,96,256]{2,1,0:T(8,128)(2,1)S(1)}, u32[]{:S(2)}) copy-start(bf16[4,96,256]{2,1,0:T(8,128)(2,1)S(1)} %collective-permute-done.4.refs_2_) | copy-start | bytes 589828
  57.3 12.2 %collective-permute-start.9 = (bf16[4,96,256]{2,1,0:T(8,128)(2,1)}, bf16[4,96,256]{2,1,0:T(8,128)(2,1)S(1)}, u32[]{:S(2)}, u32[]{:S(2)}) collective-permute-start(bf16[4,96,256]{2,1,0:T(8,128)(2,1)} %get-tuple-element.34), channel_id=1, source_target_pairs={{0,120},{1,121},{2,122},{3,123},{4,124},{5,125},{6,126},{7,127},{8... | collective-permute-start | bytes 589832 | tf_op jit(solution)/shard_map/ppermute | solution.py:45
  57.3 12.2 %copy-start.7 = (bf16[4,96,256]{2,1,0:T(8,128)(2,1)}, bf16[4,96,256]{2,1,0:T(8,128)(2,1)S(1)}, u32[]{:S(2)}) copy-start(bf16[4,96,256]{2,1,0:T(8,128)(2,1)S(1)} %collective-permute-done.5.refs_3_) | copy-start | bytes 589828
  57.3 12.2 %copy-start.9 = (bf16[4,96,256]{2,1,0:T(8,128)(2,1)}, bf16[4,96,256]{2,1,0:T(8,128)(2,1)S(1)}, u32[]{:S(2)}) copy-start(bf16[4,96,256]{2,1,0:T(8,128)(2,1)S(1)} %collective-permute-done.6.refs_4_) | copy-start | bytes 589828
  72.5 8.0 %collective-permute-start.10 = (bf16[4,96,256]{2,1,0:T(8,128)(2,1)}, bf16[4,96,256]{2,1,0:T(8,128)(2,1)S(1)}, u32[]{:S(2)}, u32[]{:S(2)}) collective-permute-start(bf16[4,96,256]{2,1,0:T(8,128)(2,1)} %get-tuple-element.36), channel_id=1, source_target_pairs={{0,2},{1,3},{2,4},{3,5},{4,6},{5,7},{6,0},{7,1},{8,10},{9,11},{10,... | collective-permute-start | bytes 589832 | tf_op jit(solution)/shard_map/ppermute | solution.py:50
  72.6 8.8 %collective-permute-start.11 = (bf16[4,96,256]{2,1,0:T(8,128)(2,1)}, bf16[4,96,256]{2,1,0:T(8,128)(2,1)S(1)}, u32[]{:S(2)}, u32[]{:S(2)}) collective-permute-start(bf16[4,96,256]{2,1,0:T(8,128)(2,1)} %get-tuple-element.37), channel_id=1, source_target_pairs={{0,4},{1,5},{2,6},{3,7},{4,0},{5,1},{6,2},{7,3},{8,12},{9,13},{10,... | collective-permute-start | bytes 589832 | tf_op jit(solution)/shard_map/ppermute | solution.py:50
  76.1 11.0 %collective-permute-start.12 = (bf16[4,96,256]{2,1,0:T(8,128)(2,1)}, bf16[4,96,256]{2,1,0:T(8,128)(2,1)S(1)}, u32[]{:S(2)}, u32[]{:S(2)}) collective-permute-start(bf16[4,96,256]{2,1,0:T(8,128)(2,1)} %get-tuple-element.38), channel_id=1, source_target_pairs={{0,6},{1,7},{2,0},{3,1},{4,2},{5,3},{6,4},{7,5},{8,14},{9,15},{10,... | collective-permute-start | bytes 589832 | tf_op jit(solution)/shard_map/ppermute | solution.py:50
  76.7 16.3 %collective-permute-start.13 = (bf16[4,96,256]{2,1,0:T(8,128)(2,1)}, bf16[4,96,256]{2,1,0:T(8,128)(2,1)S(1)}, u32[]{:S(2)}, u32[]{:S(2)}) collective-permute-start(bf16[4,96,256]{2,1,0:T(8,128)(2,1)} %get-tuple-element.39), channel_id=1, source_target_pairs={{0,8},{1,9},{2,10},{3,11},{4,12},{5,13},{6,14},{7,15},{8,0},{9,1},... | collective-permute-start | bytes 589832 | tf_op jit(solution)/shard_map/ppermute | solution.py:50
  76.7 16.3 %collective-permute-start.14 = (bf16[4,96,256]{2,1,0:T(8,128)(2,1)}, bf16[4,96,256]{2,1,0:T(8,128)(2,1)S(1)}, u32[]{:S(2)}, u32[]{:S(2)}) collective-permute-start(bf16[4,96,256]{2,1,0:T(8,128)(2,1)} %get-tuple-element.40), channel_id=1, source_target_pairs={{0,10},{1,11},{2,12},{3,13},{4,14},{5,15},{6,8},{7,9},{8,2},{9,3},... | collective-permute-start | bytes 589832 | tf_op jit(solution)/shard_map/ppermute | solution.py:50
  80.5 12.5 %copy-start.6 = (bf16[4,96,256]{2,1,0:T(8,128)(2,1)}, bf16[4,96,256]{2,1,0:T(8,128)(2,1)S(1)}, u32[]{:S(2)}) copy-start(bf16[4,96,256]{2,1,0:T(8,128)(2,1)S(1)} %collective-permute-done.10.refs_1_) | copy-start | bytes 589828
  80.5 12.5 %collective-permute-start.15 = (bf16[4,96,256]{2,1,0:T(8,128)(2,1)}, bf16[4,96,256]{2,1,0:T(8,128)(2,1)S(1)}, u32[]{:S(2)}, u32[]{:S(2)}) collective-permute-start(bf16[4,96,256]{2,1,0:T(8,128)(2,1)} %get-tuple-element.41), channel_id=1, source_target_pairs={{0,12},{1,13},{2,14},{3,15},{4,8},{5,9},{6,10},{7,11},{8,4},{9,5},... | collective-permute-start | bytes 589832 | tf_op jit(solution)/shard_map/ppermute | solution.py:50
  81.4 11.7 %copy-start.8 = (bf16[4,96,256]{2,1,0:T(8,128)(2,1)}, bf16[4,96,256]{2,1,0:T(8,128)(2,1)S(1)}, u32[]{:S(2)}) copy-start(bf16[4,96,256]{2,1,0:T(8,128)(2,1)S(1)} %collective-permute-done.11.refs_2_) | copy-start | bytes 589828
  81.4 11.6 %collective-permute-start.16 = (bf16[4,96,256]{2,1,0:T(8,128)(2,1)}, bf16[4,96,256]{2,1,0:T(8,128)(2,1)S(1)}, u32[]{:S(2)}, u32[]{:S(2)}) collective-permute-start(bf16[4,96,256]{2,1,0:T(8,128)(2,1)} %get-tuple-element.42), channel_id=1, source_target_pairs={{0,14},{1,15},{2,8},{3,9},{4,10},{5,11},{6,12},{7,13},{8,6},{9,7},... | collective-permute-start | bytes 589832 | tf_op jit(solution)/shard_map/ppermute | solution.py:50
  87.1 5.9 %copy-start.11 = (bf16[4,96,256]{2,1,0:T(8,128)(2,1)}, bf16[4,96,256]{2,1,0:T(8,128)(2,1)S(1)}, u32[]{:S(2)}) copy-start(bf16[4,96,256]{2,1,0:T(8,128)(2,1)S(1)} %collective-permute-done.12.refs_3_) | copy-start | bytes 589828
  103.5 6.1 %collective-permute-start.17 = (bf16[8,768]{1,0:T(8,128)(2,1)S(1)}, bf16[8,768]{1,0:T(8,128)(2,1)S(1)}, u32[]{:S(2)}, u32[]{:S(2)}) collective-permute-start(bf16[8,768]{1,0:T(8,128)(2,1)S(1)} %pad_maximum_fusion.1), channel_id=1, source_target_pairs={{0,1},{1,0},{2,3},{3,2},{4,5},{5,4},{6,7},{7,6},{8,9},{9,8},{10,11... | collective-permute-start | bytes 36872 | tf_op jit(solution)/shard_map/ppermute | solution.py:370
  103.6 33.4 %all-to-all-start.1 = ((bf16[8,4,96,256]{3,2,1,0:T(8,128)(2,1)}), bf16[8,4,96,256]{3,2,1,0:T(8,128)(2,1)S(1)}, u32[]{:S(2)}, u32[]{:S(2)}) async-start(bf16[8,4,96,256]{3,2,1,0:T(8,128)(2,1)} %copy-done), calls=%async_computation.1 | async-start | bytes 3145728 | tf_op jit(solution)/shard_map/all_to_all | solution.py:322
  109.6 7.2 %collective-permute-start.18 = (bf16[8,768]{1,0:T(8,128)(2,1)S(1)}, bf16[8,768]{1,0:T(8,128)(2,1)S(1)}, u32[]{:S(2)}, u32[]{:S(2)}) collective-permute-start(bf16[8,768]{1,0:T(8,128)(2,1)S(1)} %fusion.8), channel_id=1, source_target_pairs={{0,8},{1,9},{2,10},{3,11},{4,12},{5,13},{6,14},{7,15},{8,0},{9,1},... | collective-permute-start | bytes 36872 | tf_op jit(solution)/shard_map/ppermute | solution.py:370
  116.8 16.3 %collective-permute-start.21 = (bf16[8,768]{1,0:T(8,128)(2,1)S(1)}, bf16[8,768]{1,0:T(8,128)(2,1)S(1)}, u32[]{:S(2)}, u32[]{:S(2)}) collective-permute-start(bf16[8,768]{1,0:T(8,128)(2,1)S(1)} %max.16), channel_id=1, source_target_pairs={{0,6},{1,7},{2,4},{3,5},{4,2},{5,3},{6,0},{7,1},{8,14},{9,15},{10,... | collective-permute-start | bytes 36872 | tf_op jit(solution)/shard_map/ppermute | solution.py:370
  130.9 5.2 %collective-permute-start.20 = (bf16[8,768]{1,0:T(8,128)(2,1)S(1)}, bf16[8,768]{1,0:T(8,128)(2,1)S(1)}, u32[]{:S(2)}, u32[]{:S(2)}) collective-permute-start(bf16[8,768]{1,0:T(8,128)(2,1)S(1)} %max.16), channel_id=1, source_target_pairs={{0,4},{1,5},{2,6},{3,7},{4,0},{5,1},{6,2},{7,3},{8,12},{9,13},{10,... | collective-permute-start | bytes 36872 | tf_op jit(solution)/shard_map/ppermute | solution.py:370
  130.9 5.2 %collective-permute-start.19 = (bf16[8,768]{1,0:T(8,128)(2,1)S(1)}, bf16[8,768]{1,0:T(8,128)(2,1)S(1)}, u32[]{:S(2)}, u32[]{:S(2)}) collective-permute-start(bf16[8,768]{1,0:T(8,128)(2,1)S(1)} %max.16), channel_id=1, source_target_pairs={{0,2},{1,3},{2,0},{3,1},{4,6},{5,7},{6,4},{7,5},{8,10},{9,11},{10,... | collective-permute-start | bytes 36872 | tf_op jit(solution)/shard_map/ppermute | solution.py:370
  (13 other events, 12.5 us)
where the time goes:
time: 143 us; the launch traced here: 142 us
  starting transfers between devices  61.5 us (43%)
  waiting for transfers between devices  44.5 us (31%)
  Pallas kernels  23.2 us (16%)
  local copies, waits for them, and re-layouts  8.9 us (6%)
  other arithmetic  3.01 us (2%)
    ppermute x7, waiting for transfers between devices, first_move(): return lax.ppermute(array, ('dev', 'ma'), pairs)  24 us
    ppermute x5, starting transfers between devices, shards(): lax.ppermute(peak, 'ma', [(j, j ^ step) for j in range(16)])  17.9 us
    all_to_all x2, starting transfers between devices, exchange(): lax.all_to_all(array, ('dev', 'ma'), 0, 0, tiled=True, axis_index_groups=...  16.8 us
    ppermute x7, starting transfers between devices, first_move(): return lax.ppermute(array, ('dev', 'ma'), pairs)  12.6 us
    pallas_call x2, Pallas kernels, prepare(): pl.pallas_call(functools.partial(prepare_body, first), grid_spec=pltpu.Pr...  10.5 us
    ppermute x7, starting transfers between devices, second_move(): return lax.ppermute(array, ('dev', 'ma'), pairs)  10.2 us
    ppermute x7, waiting for transfers between devices, second_move(): return lax.ppermute(array, ('dev', 'ma'), pairs)  9.44 us
    ppermute x5, waiting for transfers between devices, shards(): lax.ppermute(peak, 'ma', [(j, j ^ step) for j in range(16)])  8.69 us
  transfers between devices with their start and end apart: 24, of which 11 were waited for; matrix products, arithmetic and copies ran while one was open for 2% of the time, Pallas kernels for 12%

commit v1 on v0

--- a/solution.py
+++ b/solution.py
@@ -17,6 +17,7 @@
 SIZES = (4, 4)
 WHOLE = (False, True)
 SIDE = 4
+STEP = 2
 PLACES = 8
 
 
@@ -70,28 +71,30 @@
 def prepare_body(first, place_ref, pick_ref, gain_ref, own_ref, other_ref, *refs):
     out_refs = refs[:-1]
     turned_ref = refs[-1]
-    width = own_ref.shape[1]
+    count, width, _ = own_ref.shape
     contract = (((1,), (1,)), ((), ()))
-
-    def turned(ref):
-        rows = lax.dot_general(pick_ref[...], ref[0], contract, preferred_element_type=jnp.float32)
-        return rows.reshape(KV_HEADS * SLOTS, -1, width)
-
-    both = jnp.concatenate([turned(own_ref), turned(other_ref)], axis=1)
-    both = both.reshape(-1, width)
-    if len(out_refs) == 1:
-        both = both * gain_ref[pl.ds(first + pl.program_id(0), 1), :]
-    turned_ref[...] = both.astype(jnp.bfloat16)
-    rows = turned_ref.shape[0] // KV_HEADS
-    if len(out_refs) == 1:
-        out_refs[0][:, 0] = turned_ref[...].reshape(KV_HEADS, rows, width)
-        return
+    rows = turned_ref.shape[1] // KV_HEADS
     a = place_ref[1]
     y = place_ref[2]
-    for s in range(2):
-        for r in range(SIDE):
-            g = (a ^ s) * SIDE + ((y + r) & (SIDE - 1))
-            out_refs[s * SIDE + r][0] = turned_ref[pl.ds(pl.multiple_of(g * rows, 16), rows), :]
+
+    def turned(block):
+        found = lax.dot_general(pick_ref[...], block, contract, preferred_element_type=jnp.float32)
+        return found.reshape(KV_HEADS * SLOTS, -1, width)
+
+    for n in range(count):
+        both = jnp.concatenate([turned(own_ref[n]), turned(other_ref[n])], axis=1)
+        both = both.reshape(-1, width)
+        if len(out_refs) == 1:
+            layer = first + pl.program_id(0) * count + n
+            both = both * gain_ref[pl.ds(layer, 1), :]
+            out_refs[0][:, n] = both.astype(jnp.bfloat16).reshape(KV_HEADS, rows, width)
+        else:
+            turned_ref[n] = both.astype(jnp.bfloat16)
+            for s in range(2):
+                for r in range(SIDE):
+                    g = (a ^ s) * SIDE + ((y + r) & (SIDE - 1))
+                    start = pl.multiple_of(g * rows, 16)
+                    out_refs[s * SIDE + r][n] = turned_ref[n, pl.ds(start, rows), :]
 
 
 def prepare(stored, other, gain, place, first, whole):
@@ -99,25 +102,26 @@
     layers = other.shape[0]
     width = features // 2
     rows = 2 * columns // KV_HEADS
+    step = STEP
     if whole:
-        out_specs = [pl.BlockSpec((PLACES, 1, rows, width), lambda l, place: (0, l, 0, 0))]
+        out_specs = [pl.BlockSpec((PLACES, step, rows, width), lambda l, place: (0, l, 0, 0))]
         out_shape = [jax.ShapeDtypeStruct((PLACES, layers, rows, width), jnp.bfloat16)]
     else:
-        out_specs = [pl.BlockSpec((1, rows, width), lambda l, place: (l, 0, 0))] * PLACES
+        out_specs = [pl.BlockSpec((step, rows, width), lambda l, place: (l, 0, 0))] * PLACES
         out_shape = [jax.ShapeDtypeStruct((layers, rows, width), jnp.bfloat16)] * PLACES
     return pl.pallas_call(
         functools.partial(prepare_body, first),
         grid_spec=pltpu.PrefetchScalarGridSpec(
             num_scalar_prefetch=1,
-            grid=(layers,),
+            grid=(layers // step,),
             in_specs=[
                 pl.BlockSpec((columns, columns), lambda l, place: (0, 0)),
                 pl.BlockSpec(gain.shape, lambda l, place: (0, 0)),
-                pl.BlockSpec((1, width, columns), lambda l, place: (first + l, place[0], 0)),
-                pl.BlockSpec((1, width, columns), lambda l, place: (l, 0, 0)),
+                pl.BlockSpec((step, width, columns), lambda l, place: (first // step + l, place[0], 0)),
+                pl.BlockSpec((step, width, columns), lambda l, place: (l, 0, 0)),
             ],
             out_specs=out_specs,
-            scratch_shapes=[pltpu.VMEM((2 * columns, width), jnp.bfloat16)],
+            scratch_shapes=[pltpu.VMEM((step, 2 * columns, width), jnp.bfloat16)],
         ),
         out_shape=out_shape,
         name="prepare",
@@ -322,12 +326,14 @@
     return lax.all_to_all(array, ("dev", "ma"), 0, 0, tiled=True, axis_index_groups=groups)
 
 
-STAGE = ((1, 0), (3, 0), (2, 0), (0, 1), (1, 1), (3, 1), (2, 1))
-
-
-def staged(buffers, move):
+STAGE = ((2, 1), (1, 1), (3, 1), (0, 1), (2, 0), (1, 0), (3, 0))
+
+LAST = ((2, 1), (1, 0), (2, 0), (0, 1), (3, 1), (3, 0), (1, 1))
+
+
+def staged(buffers, move, order):
     out = list(buffers)
-    for step, s in STAGE:
+    for step, s in order:
         k = s * SIDE + step
         out[k] = move(buffers[k], step, s)
     return out
@@ -349,7 +355,7 @@
         )
         theirs = swap(theirs)
         blocks = prepare(joined_weight, theirs, gain if whole else norm_gain, place, first, whole)
-        moved.append([exchange(blocks[0], FIRST_GROUPS)] if whole else staged(blocks, first_move))
+        moved.append([exchange(blocks[0], FIRST_GROUPS)] if whole else staged(blocks, first_move, STAGE))
     outs = []
     found = []
     for first, buffers, whole in zip(firsts, moved, WHOLE):
@@ -360,14 +366,16 @@
         if whole:
             arrived = [exchange(buffers[0], SECOND_GROUPS)]
         else:
-            arrived = staged(buffers, second_move)
+            arrived = staged(buffers, second_move, LAST)
         own = None if whole else norm_gain
         outs = list(finish(arrived, turns[whole], own, layers, first, outs))
         if not whole:
             found.append(outs.pop()[:, 0].astype(jnp.bfloat16))
     peak = jnp.concatenate(found, axis=0)
     for steps in JOINS:
-        others = [lax.ppermute(peak, "ma", [(j, j ^ step) for j in range(16)]) for step in steps]
+        others = [
+            lax.ppermute(peak, "ma", [(j, j ^ step) for j in range(16)]) for step in steps
+        ]
         for other in others:
             peak = jnp.maximum(peak, other)
     ready, stored = peak[: SIZES[0]], peak[SIZES[0] :].reshape(-1, SLOTS, dim)

time: 143 us -> 142 us (level)
  Pallas kernels: 23.2 us -> 20.8 us
    pallas_call x2, Pallas kernels: 10.5 us -> 8.12 us  [prepare(): pl.pallas_call(functools.partial(prepare_body, first), grid_spec=pltpu.Pr...]
  transfers between devices with their start and end apart: 24 -> 24, of which waited for: 11 -> 11; matrix products, arithmetic and copies ran while one was open for 2% -> 2% of each run, Pallas kernels for 12% -> 10%
where the time goes in v1:
time: 142 us; the launch traced here: 141 us
  starting transfers between devices  61.5 us (43%)
  waiting for transfers between devices  45.7 us (32%)
  Pallas kernels  20.8 us (15%)
  local copies, waits for them, and re-layouts  8.9 us (6%)
  other arithmetic  3.01 us (2%)
    ppermute x7, waiting for transfers between devices, first_move(): return lax.ppermute(array, ('dev', 'ma'), pairs)  25.1 us
    ppermute x5, starting transfers between devices, shards(): lax.ppermute(peak, 'ma', [(j, j ^ step) for j in range(16)])  17.9 us
    all_to_all x2, starting transfers between devices, exchange(): lax.all_to_all(array, ('dev', 'ma'), 0, 0, tiled=True, axis_index_groups=...  16.8 us
    ppermute x7, starting transfers between devices, first_move(): return lax.ppermute(array, ('dev', 'ma'), pairs)  12.6 us
    ppermute x7, starting transfers between devices, second_move(): return lax.ppermute(array, ('dev', 'ma'), pairs)  10.1 us
    ppermute x7, waiting for transfers between devices, second_move(): return lax.ppermute(array, ('dev', 'ma'), pairs)  9.49 us
    ppermute x5, waiting for transfers between devices, shards(): lax.ppermute(peak, 'ma', [(j, j ^ step) for j in range(16)])  8.69 us
    pallas_call x2, Pallas kernels, finish(): pl.pallas_call(body, grid=(layers,), in_specs=in_specs + held + [pl.Block...  8.16 us
  transfers between devices with their start and end apart: 24, of which 11 were waited for; matrix products, arithmetic and copies ran while one was open for 2% of the time, Pallas kernels for 10%

profile of v1, /device:TPU:2, one launch (start us, length us, event | category | flops | bytes accessed | tf_op | source)
XLA Modules:
  0.0 141.0 jit_solution(17720887245461241173)
XLA Ops:
  0.7 1.6 %constant_dynamic-slice_fusion = (bf16[4,256,384]{2,1,0:T(8,128)(2,1)S(1)}, bf16[4,256,384]{2,1,0:T(8,128)(2,1)S(1)}) fusion(bf16[8,512,384]{2,1,0:T(8,128)(2,1)} %own_ref.3, s32[]{:T(128)S(6)} %select_n.44), kind=kLoop, calls=%fused_computation.33 | loop fusion | bytes 3145732 | tf_op jit(solution)/shard_map/dynamic_slice | solution.py:353
  2.8 3.4 %collective-permute-start = (f32[8,256]{1,0:T(8,128)S(1)}, f32[8,256]{1,0:T(8,128)S(1)}, u32[]{:S(2)}, u32[]{:S(2)}) collective-permute-start(f32[8,256]{1,0:T(8,128)S(1)} %copy-done.18), channel_id=1, source_target_pairs={{0,0},{1,1},{2,16},{3,17},{4,32},{5,33},{6,48},{7,49},{8,64},{9,65... | collective-permute-start | bytes 24584 | tf_op jit(solution)/shard_map/ppermute | solution.py:41
  6.9 2.4 %collective-permute-done.gain_ref = f32[8,256]{1,0:T(8,128)S(1)} collective-permute-done((f32[8,256]{1,0:T(8,128)S(1)}, f32[8,256]{1,0:T(8,128)S(1)}, u32[]{:S(2)}, u32[]{:S(2)}) %collective-permute-start) | collective-permute-done | bytes 8224 | tf_op jit(solution)/shard_map/ppermute | solution.py:41
  10.7 4.1 %prepare.2 = bf16[8,4,96,256]{3,2,1,0:T(8,128)(2,1)} custom-call(s32[3]{0:T(128)} %pad_add_fusion.1.place_ref, bf16[384,384]{1,0:T(8,128)(2,1)} %constant.73.clone.pick_ref, f32[8,256]{1,0:T(8,128)} %copy-done.19, bf16[8,512,384]{2,1,0:T(8,128)(2,1)} %own_ref.3, bf16[4,256,384]{2,1,0:T(8,128)(2,1)} %copy-done.3), custom_call_target="tpu_custom_call" | custom-call | tf_op jit(solution)/shard_map/prepare/pallas_call | solution.py:112
  14.8 10.8 %all-to-all-start = ((bf16[8,4,96,256]{3,2,1,0:T(8,128)(2,1)}), bf16[8,4,96,256]{3,2,1,0:T(8,128)(2,1)S(1)}, u32[]{:S(2)}, u32[]{:S(2)}) async-start(bf16[8,4,96,256]{3,2,1,0:T(8,128)(2,1)} %prepare.2), calls=%async_computation | async-start | bytes 3145728 | tf_op jit(solution)/shard_map/all_to_all | solution.py:326
  26.5 4.0 %prepare.3 = (bf16[4,96,256]{2,1,0:T(8,128)(2,1)}, bf16[4,96,256]{2,1,0:T(8,128)(2,1)}, bf16[4,96,256]{2,1,0:T(8,128)(2,1)}, bf16[4,96,256]{2,1,0:T(8,128)(2,1)}...) custom-call(s32[3]{0:T(128)} %pad_add_fusion.1.place_ref, ...), custom_call_target="tpu_custom_call" | custom-call | tf_op jit(solution)/shard_map/prepare/pallas_call | solution.py:112
  30.5 2.1 %collective-permute-start.3 = (bf16[4,96,256]{2,1,0:T(8,128)(2,1)}, bf16[4,96,256]{2,1,0:T(8,128)(2,1)S(1)}, u32[]{:S(2)}, u32[]{:S(2)}) collective-permute-start(bf16[4,96,256]{2,1,0:T(8,128)(2,1)} %get-tuple-element.28), channel_id=1, source_target_pairs={{0,16},{1,17},{2,18},{3,19},{4,20},{5,21},{6,22},{7,23},{8,24},{9,... | collective-permute-start | bytes 589832 | tf_op jit(solution)/shard_map/ppermute | solution.py:46
  32.6 2.7 %collective-permute-start.4 = (bf16[4,96,256]{2,1,0:T(8,128)(2,1)}, bf16[4,96,256]{2,1,0:T(8,128)(2,1)S(1)}, u32[]{:S(2)}, u32[]{:S(2)}) collective-permute-start(bf16[4,96,256]{2,1,0:T(8,128)(2,1)} %get-tuple-element.29), channel_id=1, source_target_pairs={{0,32},{1,33},{2,34},{3,35},{4,36},{5,37},{6,38},{7,39},{8,40},{9,... | collective-permute-start | bytes 589832 | tf_op jit(solution)/shard_map/ppermute | solution.py:46
  35.3 1.5 %collective-permute-start.5 = (bf16[4,96,256]{2,1,0:T(8,128)(2,1)}, bf16[4,96,256]{2,1,0:T(8,128)(2,1)S(1)}, u32[]{:S(2)}, u32[]{:S(2)}) collective-permute-start(bf16[4,96,256]{2,1,0:T(8,128)(2,1)} %get-tuple-element.30), channel_id=1, source_target_pairs={{0,48},{1,49},{2,50},{3,51},{4,52},{5,53},{6,54},{7,55},{8,56},{9,... | collective-permute-start | bytes 589832 | tf_op jit(solution)/shard_map/ppermute | solution.py:46
  36.8 2.7 %collective-permute-start.6 = (bf16[4,96,256]{2,1,0:T(8,128)(2,1)}, bf16[4,96,256]{2,1,0:T(8,128)(2,1)S(1)}, u32[]{:S(2)}, u32[]{:S(2)}) collective-permute-start(bf16[4,96,256]{2,1,0:T(8,128)(2,1)} %get-tuple-element.31), channel_id=1, source_target_pairs={{0,72},{1,73},{2,74},{3,75},{4,76},{5,77},{6,78},{7,79},{8,64},{9,... | collective-permute-start | bytes 589832 | tf_op jit(solution)/shard_map/ppermute | solution.py:46
  40.1 11.8 %collective-permute-done.3.refs_1_ = bf16[4,96,256]{2,1,0:T(8,128)(2,1)S(1)} collective-permute-done((bf16[4,96,256]{2,1,0:T(8,128)(2,1)}, bf16[4,96,256]{2,1,0:T(8,128)(2,1)S(1)}, u32[]{:S(2)}, u32[]{:S(2)}) %collective-permute-start.3) | collective-permute-done | bytes 196640 | tf_op jit(solution)/shard_map/ppermute | solution.py:46
  51.9 3.1 %collective-permute-start.8 = (bf16[4,96,256]{2,1,0:T(8,128)(2,1)}, bf16[4,96,256]{2,1,0:T(8,128)(2,1)S(1)}, u32[]{:S(2)}, u32[]{:S(2)}) collective-permute-start(bf16[4,96,256]{2,1,0:T(8,128)(2,1)} %get-tuple-element.33), channel_id=1, source_target_pairs={{0,104},{1,105},{2,106},{3,107},{4,108},{5,109},{6,110},{7,111},{8... | collective-permute-start | bytes 589832 | tf_op jit(solution)/shard_map/ppermute | solution.py:46
  54.9 1.1 collective-permute-done.4.refs_2_
  56.2 11.3 %collective-permute-done.7.refs_5_ = bf16[4,96,256]{2,1,0:T(8,128)(2,1)S(1)} collective-permute-done((bf16[4,96,256]{2,1,0:T(8,128)(2,1)}, bf16[4,96,256]{2,1,0:T(8,128)(2,1)S(1)}, u32[]{:S(2)}, u32[]{:S(2)}) %collective-permute-start.7) | collective-permute-done | bytes 196640 | tf_op jit(solution)/shard_map/ppermute | solution.py:46
  69.0 2.3 %reorder.1 = (bf16[4,96,256]{2,1,0:T(8,128)(2,1)}, bf16[4,96,256]{2,1,0:T(8,128)(2,1)}, bf16[4,96,256]{2,1,0:T(8,128)(2,1)}, bf16[4,96,256]{2,1,0:T(8,128)(2,1)}...) custom-call(bf16[4,96,256]{2,1,0:T(8,128)(2,1)} %get-tuple-element.2, ...), custom_call_target="tpu_custom_call" | custom-call | tf_op jit(solution)/shard_map/reorder/pallas_call | solution.py:159
  71.4 2.8 %collective-permute-start.11 = (bf16[4,96,256]{2,1,0:T(8,128)(2,1)}, bf16[4,96,256]{2,1,0:T(8,128)(2,1)S(1)}, u32[]{:S(2)}, u32[]{:S(2)}) collective-permute-start(bf16[4,96,256]{2,1,0:T(8,128)(2,1)} %get-tuple-element.37), channel_id=1, source_target_pairs={{0,4},{1,5},{2,6},{3,7},{4,0},{5,1},{6,2},{7,3},{8,12},{9,13},{10,... | collective-permute-start | bytes 589832 | tf_op jit(solution)/shard_map/ppermute | solution.py:51
  75.5 3.0 %collective-permute-start.14 = (bf16[4,96,256]{2,1,0:T(8,128)(2,1)}, bf16[4,96,256]{2,1,0:T(8,128)(2,1)S(1)}, u32[]{:S(2)}, u32[]{:S(2)}) collective-permute-start(bf16[4,96,256]{2,1,0:T(8,128)(2,1)} %get-tuple-element.40), channel_id=1, source_target_pairs={{0,10},{1,11},{2,12},{3,13},{4,14},{5,15},{6,8},{7,9},{8,2},{9,3},... | collective-permute-start | bytes 589832 | tf_op jit(solution)/shard_map/ppermute | solution.py:51
  78.4 0.9 collective-permute-done.10.refs_1_
  80.2 3.2 %collective-permute-start.16 = (bf16[4,96,256]{2,1,0:T(8,128)(2,1)}, bf16[4,96,256]{2,1,0:T(8,128)(2,1)S(1)}, u32[]{:S(2)}, u32[]{:S(2)}) collective-permute-start(bf16[4,96,256]{2,1,0:T(8,128)(2,1)} %get-tuple-element.42), channel_id=1, source_target_pairs={{0,14},{1,15},{2,8},{3,9},{4,10},{5,11},{6,12},{7,13},{8,6},{9,7},... | collective-permute-start | bytes 589832 | tf_op jit(solution)/shard_map/ppermute | solution.py:51
  83.5 2.4 %collective-permute-done.12.refs_3_ = bf16[4,96,256]{2,1,0:T(8,128)(2,1)S(1)} collective-permute-done((bf16[4,96,256]{2,1,0:T(8,128)(2,1)}, bf16[4,96,256]{2,1,0:T(8,128)(2,1)S(1)}, u32[]{:S(2)}, u32[]{:S(2)}) %collective-permute-start.12) | collective-permute-done | bytes 196640 | tf_op jit(solution)/shard_map/ppermute | solution.py:51
  85.9 5.8 %collective-permute-done.13.refs_4_ = bf16[4,96,256]{2,1,0:T(8,128)(2,1)S(1)} collective-permute-done((bf16[4,96,256]{2,1,0:T(8,128)(2,1)}, bf16[4,96,256]{2,1,0:T(8,128)(2,1)S(1)}, u32[]{:S(2)}, u32[]{:S(2)}) %collective-permute-start.13) | collective-permute-done | bytes 196640 | tf_op jit(solution)/shard_map/ppermute | solution.py:51
  92.7 4.1 %finish.2 = (bf16[8,512,256]{2,1,0:T(8,128)(2,1)}, bf16[8,128,256]{2,1,0:T(8,128)(2,1)}, bf16[8,128,256]{2,1,0:T(8,128)(2,1)}, f32[4,1,768]{2,1,0:T(1,128)}) custom-call(bf16[2,128,128]{2,1,0:T(8,128)(2,1)} %get-tuple-element.54.turn_ref, f32[8,256]{1,0:T(8,128)} %gain_ref.3, bf16[4,96,256]{2,1,0:T(8,128)(2,1)} %get-tuple-element.35.refs_0_, ...), custom_call_target="tpu_custom_call" | custom-call | tf_op jit(solution)/shard_map/finish/pallas_call | solution.py:286
  97.5 1.2 copy-done
  98.7 2.3 %peaks.1 = f32[2,384]{1,0:T(2,128)} custom-call(bf16[8,4,96,256]{3,2,1,0:T(8,128)(2,1)} %copy-done, bf16[8,4,96,256]{3,2,1,0:T(8,128)(2,1)} %copy-done, bf16[8,4,96,256]{3,2,1,0:T(8,128)(2,1)} %copy-done, bf16[8,4,96,256]{3,2,1,0:T(8,128)(2,1)} %copy-done, bf16[8,4,96,256]{3,2,1,0:T(8,128)(2,1)} %copy-done, bf16[8,4,96,256]{3,2,1,0:T(8,128)(2,1)} %copy-done, ...), custom_call_target="tpu_custom_call" | custom-call | tf_op jit(solution)/shard_map/peaks/pallas_call | solution.py:194
  102.4 6.0 %all-to-all-start.1 = ((bf16[8,4,96,256]{3,2,1,0:T(8,128)(2,1)}), bf16[8,4,96,256]{3,2,1,0:T(8,128)(2,1)S(1)}, u32[]{:S(2)}, u32[]{:S(2)}) async-start(bf16[8,4,96,256]{3,2,1,0:T(8,128)(2,1)} %copy-done), calls=%async_computation.1 | async-start | bytes 3145728 | tf_op jit(solution)/shard_map/all_to_all | solution.py:326
  108.4 1.6 %collective-permute-start.18 = (bf16[8,768]{1,0:T(8,128)(2,1)S(1)}, bf16[8,768]{1,0:T(8,128)(2,1)S(1)}, u32[]{:S(2)}, u32[]{:S(2)}) collective-permute-start(bf16[8,768]{1,0:T(8,128)(2,1)S(1)} %fusion.8), channel_id=1, source_target_pairs={{0,8},{1,9},{2,10},{3,11},{4,12},{5,13},{6,14},{7,15},{8,0},{9,1},... | collective-permute-start | bytes 36872 | tf_op jit(solution)/shard_map/ppermute | solution.py:377
  110.0 5.6 %collective-permute-done.18 = bf16[8,768]{1,0:T(8,128)(2,1)S(1)} collective-permute-done((bf16[8,768]{1,0:T(8,128)(2,1)S(1)}, bf16[8,768]{1,0:T(8,128)(2,1)S(1)}, u32[]{:S(2)}, u32[]{:S(2)}) %collective-permute-start.18) | collective-permute-done | bytes 12320 | tf_op jit(solution)/shard_map/ppermute | solution.py:377
  115.6 14.1 %collective-permute-start.21 = (bf16[8,768]{1,0:T(8,128)(2,1)S(1)}, bf16[8,768]{1,0:T(8,128)(2,1)S(1)}, u32[]{:S(2)}, u32[]{:S(2)}) collective-permute-start(bf16[8,768]{1,0:T(8,128)(2,1)S(1)} %max.16), channel_id=1, source_target_pairs={{0,6},{1,7},{2,4},{3,5},{4,2},{5,3},{6,0},{7,1},{8,14},{9,15},{10,... | collective-permute-start | bytes 36872 | tf_op jit(solution)/shard_map/ppermute | solution.py:377
  129.7 2.2 %collective-permute-start.19 = (bf16[8,768]{1,0:T(8,128)(2,1)S(1)}, bf16[8,768]{1,0:T(8,128)(2,1)S(1)}, u32[]{:S(2)}, u32[]{:S(2)}) collective-permute-start(bf16[8,768]{1,0:T(8,128)(2,1)S(1)} %max.16), channel_id=1, source_target_pairs={{0,2},{1,3},{2,0},{3,1},{4,6},{5,7},{6,4},{7,5},{8,10},{9,11},{10,... | collective-permute-start | bytes 36872 | tf_op jit(solution)/shard_map/ppermute | solution.py:377
  131.9 3.0 %collective-permute-done.20 = bf16[8,768]{1,0:T(8,128)(2,1)S(1)} collective-permute-done((bf16[8,768]{1,0:T(8,128)(2,1)S(1)}, bf16[8,768]{1,0:T(8,128)(2,1)S(1)}, u32[]{:S(2)}, u32[]{:S(2)}) %collective-permute-start.20) | collective-permute-done | bytes 12320 | tf_op jit(solution)/shard_map/ppermute | solution.py:377
  135.8 1.2 copy-done.1
  137.0 4.0 %finish.3 = (bf16[8,512,256]{2,1,0:T(8,128)(2,1)}, bf16[8,128,256]{2,1,0:T(8,128)(2,1)}, bf16[8,128,256]{2,1,0:T(8,128)(2,1)}) custom-call(bf16[2,128,128]{2,1,0:T(8,128)(2,1)} %get-tuple-element.55.turn_ref, bf16[8,4,96,256]{3,2,1,0:T(8,128)(2,1)} %copy-done.1, ...), custom_call_target="tpu_custom_call", output_to_operand_aliasing={{0}: (9, {}), {1}: (10, {}), {2}: (11, {})} | custom-call | tf_op jit(solution)/shard_map/finish/pallas_call | solution.py:286
  (92 shorter events, 11.7 us)
Async XLA Ops:
  2.2 7.0 %collective-permute-start.1 = (bf16[4,256,384]{2,1,0:T(8,128)(2,1)S(1)}, bf16[4,256,384]{2,1,0:T(8,128)(2,1)S(1)}, u32[]{:S(2)}, u32[]{:S(2)}) collective-permute-start(bf16[4,256,384]{2,1,0:T(8,128)(2,1)S(1)} %get-tuple-element.51), channel_id=1, source_target_pairs={{0,1},{1,0},{2,3},{3,2},{4,5},{5,4},{6,7},{7,6},{8,9},{9,8},{10,11... | collective-permute-start | bytes 2359304 | tf_op jit(solution)/shard_map/ppermute | solution.py:36
  2.3 23.3 %collective-permute-start.2 = (bf16[4,256,384]{2,1,0:T(8,128)(2,1)S(1)}, bf16[4,256,384]{2,1,0:T(8,128)(2,1)S(1)}, u32[]{:S(2)}, u32[]{:S(2)}) collective-permute-start(bf16[4,256,384]{2,1,0:T(8,128)(2,1)S(1)} %get-tuple-element.50), channel_id=1, source_target_pairs={{0,1},{1,0},{2,3},{3,2},{4,5},{5,4},{6,7},{7,6},{8,9},{9,8},{10,11... | collective-permute-start | bytes 2359304 | tf_op jit(solution)/shard_map/ppermute | solution.py:36
  2.8 6.4 %collective-permute-start = (f32[8,256]{1,0:T(8,128)S(1)}, f32[8,256]{1,0:T(8,128)S(1)}, u32[]{:S(2)}, u32[]{:S(2)}) collective-permute-start(f32[8,256]{1,0:T(8,128)S(1)} %copy-done.18), channel_id=1, source_target_pairs={{0,0},{1,1},{2,16},{3,17},{4,32},{5,33},{6,48},{7,49},{8,64},{9,65... | collective-permute-start | bytes 24584 | tf_op jit(solution)/shard_map/ppermute | solution.py:41
  14.8 82.7 %all-to-all-start = ((bf16[8,4,96,256]{3,2,1,0:T(8,128)(2,1)}), bf16[8,4,96,256]{3,2,1,0:T(8,128)(2,1)S(1)}, u32[]{:S(2)}, u32[]{:S(2)}) async-start(bf16[8,4,96,256]{3,2,1,0:T(8,128)(2,1)} %prepare.2), calls=%async_computation | async-start | bytes 3145728 | tf_op jit(solution)/shard_map/all_to_all | solution.py:326
  25.6 30.5 %copy-start.20 = (s32[128]{0:T(128)S(1)}, s32[128]{0:T(128)}, u32[]{:S(2)}) copy-start(s32[128]{0:T(128)} %param.7) | copy-start | bytes 1540
  30.5 21.3 %collective-permute-start.3 = (bf16[4,96,256]{2,1,0:T(8,128)(2,1)}, bf16[4,96,256]{2,1,0:T(8,128)(2,1)S(1)}, u32[]{:S(2)}, u32[]{:S(2)}) collective-permute-start(bf16[4,96,256]{2,1,0:T(8,128)(2,1)} %get-tuple-element.28), channel_id=1, source_target_pairs={{0,16},{1,17},{2,18},{3,19},{4,20},{5,21},{6,22},{7,23},{8,24},{9,... | collective-permute-start | bytes 589832 | tf_op jit(solution)/shard_map/ppermute | solution.py:46
  32.6 23.5 %collective-permute-start.4 = (bf16[4,96,256]{2,1,0:T(8,128)(2,1)}, bf16[4,96,256]{2,1,0:T(8,128)(2,1)S(1)}, u32[]{:S(2)}, u32[]{:S(2)}) collective-permute-start(bf16[4,96,256]{2,1,0:T(8,128)(2,1)} %get-tuple-element.29), channel_id=1, source_target_pairs={{0,32},{1,33},{2,34},{3,35},{4,36},{5,37},{6,38},{7,39},{8,40},{9,... | collective-permute-start | bytes 589832 | tf_op jit(solution)/shard_map/ppermute | solution.py:46
  35.3 20.8 %collective-permute-start.5 = (bf16[4,96,256]{2,1,0:T(8,128)(2,1)}, bf16[4,96,256]{2,1,0:T(8,128)(2,1)S(1)}, u32[]{:S(2)}, u32[]{:S(2)}) collective-permute-start(bf16[4,96,256]{2,1,0:T(8,128)(2,1)} %get-tuple-element.30), channel_id=1, source_target_pairs={{0,48},{1,49},{2,50},{3,51},{4,52},{5,53},{6,54},{7,55},{8,56},{9,... | collective-permute-start | bytes 589832 | tf_op jit(solution)/shard_map/ppermute | solution.py:46
  36.8 19.3 %collective-permute-start.6 = (bf16[4,96,256]{2,1,0:T(8,128)(2,1)}, bf16[4,96,256]{2,1,0:T(8,128)(2,1)S(1)}, u32[]{:S(2)}, u32[]{:S(2)}) collective-permute-start(bf16[4,96,256]{2,1,0:T(8,128)(2,1)} %get-tuple-element.31), channel_id=1, source_target_pairs={{0,72},{1,73},{2,74},{3,75},{4,76},{5,77},{6,78},{7,79},{8,64},{9,... | collective-permute-start | bytes 589832 | tf_op jit(solution)/shard_map/ppermute | solution.py:46
  39.5 28.0 %collective-permute-start.7 = (bf16[4,96,256]{2,1,0:T(8,128)(2,1)}, bf16[4,96,256]{2,1,0:T(8,128)(2,1)S(1)}, u32[]{:S(2)}, u32[]{:S(2)}) collective-permute-start(bf16[4,96,256]{2,1,0:T(8,128)(2,1)} %get-tuple-element.32), channel_id=1, source_target_pairs={{0,88},{1,89},{2,90},{3,91},{4,92},{5,93},{6,94},{7,95},{8,80},{9,... | collective-permute-start | bytes 589832 | tf_op jit(solution)/shard_map/ppermute | solution.py:46
  51.9 16.5 %copy-start.4 = (bf16[4,96,256]{2,1,0:T(8,128)(2,1)}, bf16[4,96,256]{2,1,0:T(8,128)(2,1)S(1)}, u32[]{:S(2)}) copy-start(bf16[4,96,256]{2,1,0:T(8,128)(2,1)S(1)} %collective-permute-done.3.refs_1_) | copy-start | bytes 589828
  51.9 15.6 %collective-permute-start.8 = (bf16[4,96,256]{2,1,0:T(8,128)(2,1)}, bf16[4,96,256]{2,1,0:T(8,128)(2,1)S(1)}, u32[]{:S(2)}, u32[]{:S(2)}) collective-permute-start(bf16[4,96,256]{2,1,0:T(8,128)(2,1)} %get-tuple-element.33), channel_id=1, source_target_pairs={{0,104},{1,105},{2,106},{3,107},{4,108},{5,109},{6,110},{7,111},{8... | collective-permute-start | bytes 589832 | tf_op jit(solution)/shard_map/ppermute | solution.py:46
  56.1 12.3 %copy-start.5 = (bf16[4,96,256]{2,1,0:T(8,128)(2,1)}, bf16[4,96,256]{2,1,0:T(8,128)(2,1)S(1)}, u32[]{:S(2)}) copy-start(bf16[4,96,256]{2,1,0:T(8,128)(2,1)S(1)} %collective-permute-done.4.refs_2_) | copy-start | bytes 589828
  56.1 12.2 %collective-permute-start.9 = (bf16[4,96,256]{2,1,0:T(8,128)(2,1)}, bf16[4,96,256]{2,1,0:T(8,128)(2,1)S(1)}, u32[]{:S(2)}, u32[]{:S(2)}) collective-permute-start(bf16[4,96,256]{2,1,0:T(8,128)(2,1)} %get-tuple-element.34), channel_id=1, source_target_pairs={{0,120},{1,121},{2,122},{3,123},{4,124},{5,125},{6,126},{7,127},{8... | collective-permute-start | bytes 589832 | tf_op jit(solution)/shard_map/ppermute | solution.py:46
  56.1 12.2 %copy-start.7 = (bf16[4,96,256]{2,1,0:T(8,128)(2,1)}, bf16[4,96,256]{2,1,0:T(8,128)(2,1)S(1)}, u32[]{:S(2)}) copy-start(bf16[4,96,256]{2,1,0:T(8,128)(2,1)S(1)} %collective-permute-done.5.refs_3_) | copy-start | bytes 589828
  56.2 12.2 %copy-start.9 = (bf16[4,96,256]{2,1,0:T(8,128)(2,1)}, bf16[4,96,256]{2,1,0:T(8,128)(2,1)S(1)}, u32[]{:S(2)}) copy-start(bf16[4,96,256]{2,1,0:T(8,128)(2,1)S(1)} %collective-permute-done.6.refs_4_) | copy-start | bytes 589828
  71.3 8.0 %collective-permute-start.10 = (bf16[4,96,256]{2,1,0:T(8,128)(2,1)}, bf16[4,96,256]{2,1,0:T(8,128)(2,1)S(1)}, u32[]{:S(2)}, u32[]{:S(2)}) collective-permute-start(bf16[4,96,256]{2,1,0:T(8,128)(2,1)} %get-tuple-element.36), channel_id=1, source_target_pairs={{0,2},{1,3},{2,4},{3,5},{4,6},{5,7},{6,0},{7,1},{8,10},{9,11},{10,... | collective-permute-start | bytes 589832 | tf_op jit(solution)/shard_map/ppermute | solution.py:51
  71.4 8.8 %collective-permute-start.11 = (bf16[4,96,256]{2,1,0:T(8,128)(2,1)}, bf16[4,96,256]{2,1,0:T(8,128)(2,1)S(1)}, u32[]{:S(2)}, u32[]{:S(2)}) collective-permute-start(bf16[4,96,256]{2,1,0:T(8,128)(2,1)} %get-tuple-element.37), channel_id=1, source_target_pairs={{0,4},{1,5},{2,6},{3,7},{4,0},{5,1},{6,2},{7,3},{8,12},{9,13},{10,... | collective-permute-start | bytes 589832 | tf_op jit(solution)/shard_map/ppermute | solution.py:51
  74.9 11.0 %collective-permute-start.12 = (bf16[4,96,256]{2,1,0:T(8,128)(2,1)}, bf16[4,96,256]{2,1,0:T(8,128)(2,1)S(1)}, u32[]{:S(2)}, u32[]{:S(2)}) collective-permute-start(bf16[4,96,256]{2,1,0:T(8,128)(2,1)} %get-tuple-element.38), channel_id=1, source_target_pairs={{0,6},{1,7},{2,0},{3,1},{4,2},{5,3},{6,4},{7,5},{8,14},{9,15},{10,... | collective-permute-start | bytes 589832 | tf_op jit(solution)/shard_map/ppermute | solution.py:51
  75.5 16.3 %collective-permute-start.13 = (bf16[4,96,256]{2,1,0:T(8,128)(2,1)}, bf16[4,96,256]{2,1,0:T(8,128)(2,1)S(1)}, u32[]{:S(2)}, u32[]{:S(2)}) collective-permute-start(bf16[4,96,256]{2,1,0:T(8,128)(2,1)} %get-tuple-element.39), channel_id=1, source_target_pairs={{0,8},{1,9},{2,10},{3,11},{4,12},{5,13},{6,14},{7,15},{8,0},{9,1},... | collective-permute-start | bytes 589832 | tf_op jit(solution)/shard_map/ppermute | solution.py:51
  75.5 16.3 %collective-permute-start.14 = (bf16[4,96,256]{2,1,0:T(8,128)(2,1)}, bf16[4,96,256]{2,1,0:T(8,128)(2,1)S(1)}, u32[]{:S(2)}, u32[]{:S(2)}) collective-permute-start(bf16[4,96,256]{2,1,0:T(8,128)(2,1)} %get-tuple-element.40), channel_id=1, source_target_pairs={{0,10},{1,11},{2,12},{3,13},{4,14},{5,15},{6,8},{7,9},{8,2},{9,3},... | collective-permute-start | bytes 589832 | tf_op jit(solution)/shard_map/ppermute | solution.py:51
  79.3 12.5 %copy-start.6 = (bf16[4,96,256]{2,1,0:T(8,128)(2,1)}, bf16[4,96,256]{2,1,0:T(8,128)(2,1)S(1)}, u32[]{:S(2)}) copy-start(bf16[4,96,256]{2,1,0:T(8,128)(2,1)S(1)} %collective-permute-done.10.refs_1_) | copy-start | bytes 589828
  79.3 12.4 %collective-permute-start.15 = (bf16[4,96,256]{2,1,0:T(8,128)(2,1)}, bf16[4,96,256]{2,1,0:T(8,128)(2,1)S(1)}, u32[]{:S(2)}, u32[]{:S(2)}) collective-permute-start(bf16[4,96,256]{2,1,0:T(8,128)(2,1)} %get-tuple-element.41), channel_id=1, source_target_pairs={{0,12},{1,13},{2,14},{3,15},{4,8},{5,9},{6,10},{7,11},{8,4},{9,5},... | collective-permute-start | bytes 589832 | tf_op jit(solution)/shard_map/ppermute | solution.py:51
  80.2 11.6 %copy-start.8 = (bf16[4,96,256]{2,1,0:T(8,128)(2,1)}, bf16[4,96,256]{2,1,0:T(8,128)(2,1)S(1)}, u32[]{:S(2)}) copy-start(bf16[4,96,256]{2,1,0:T(8,128)(2,1)S(1)} %collective-permute-done.11.refs_2_) | copy-start | bytes 589828
  80.2 11.6 %collective-permute-start.16 = (bf16[4,96,256]{2,1,0:T(8,128)(2,1)}, bf16[4,96,256]{2,1,0:T(8,128)(2,1)S(1)}, u32[]{:S(2)}, u32[]{:S(2)}) collective-permute-start(bf16[4,96,256]{2,1,0:T(8,128)(2,1)} %get-tuple-element.42), channel_id=1, source_target_pairs={{0,14},{1,15},{2,8},{3,9},{4,10},{5,11},{6,12},{7,13},{8,6},{9,7},... | collective-permute-start | bytes 589832 | tf_op jit(solution)/shard_map/ppermute | solution.py:51
  85.9 5.9 %copy-start.11 = (bf16[4,96,256]{2,1,0:T(8,128)(2,1)}, bf16[4,96,256]{2,1,0:T(8,128)(2,1)S(1)}, u32[]{:S(2)}) copy-start(bf16[4,96,256]{2,1,0:T(8,128)(2,1)S(1)} %collective-permute-done.12.refs_3_) | copy-start | bytes 589828
  102.3 6.1 %collective-permute-start.17 = (bf16[8,768]{1,0:T(8,128)(2,1)S(1)}, bf16[8,768]{1,0:T(8,128)(2,1)S(1)}, u32[]{:S(2)}, u32[]{:S(2)}) collective-permute-start(bf16[8,768]{1,0:T(8,128)(2,1)S(1)} %pad_maximum_fusion.1), channel_id=1, source_target_pairs={{0,1},{1,0},{2,3},{3,2},{4,5},{5,4},{6,7},{7,6},{8,9},{9,8},{10,11... | collective-permute-start | bytes 36872 | tf_op jit(solution)/shard_map/ppermute | solution.py:377
  102.4 33.4 %all-to-all-start.1 = ((bf16[8,4,96,256]{3,2,1,0:T(8,128)(2,1)}), bf16[8,4,96,256]{3,2,1,0:T(8,128)(2,1)S(1)}, u32[]{:S(2)}, u32[]{:S(2)}) async-start(bf16[8,4,96,256]{3,2,1,0:T(8,128)(2,1)} %copy-done), calls=%async_computation.1 | async-start | bytes 3145728 | tf_op jit(solution)/shard_map/all_to_all | solution.py:326
  108.4 7.2 %collective-permute-start.18 = (bf16[8,768]{1,0:T(8,128)(2,1)S(1)}, bf16[8,768]{1,0:T(8,128)(2,1)S(1)}, u32[]{:S(2)}, u32[]{:S(2)}) collective-permute-start(bf16[8,768]{1,0:T(8,128)(2,1)S(1)} %fusion.8), channel_id=1, source_target_pairs={{0,8},{1,9},{2,10},{3,11},{4,12},{5,13},{6,14},{7,15},{8,0},{9,1},... | collective-permute-start | bytes 36872 | tf_op jit(solution)/shard_map/ppermute | solution.py:377
  115.6 16.3 %collective-permute-start.21 = (bf16[8,768]{1,0:T(8,128)(2,1)S(1)}, bf16[8,768]{1,0:T(8,128)(2,1)S(1)}, u32[]{:S(2)}, u32[]{:S(2)}) collective-permute-start(bf16[8,768]{1,0:T(8,128)(2,1)S(1)} %max.16), channel_id=1, source_target_pairs={{0,6},{1,7},{2,4},{3,5},{4,2},{5,3},{6,0},{7,1},{8,14},{9,15},{10,... | collective-permute-start | bytes 36872 | tf_op jit(solution)/shard_map/ppermute | solution.py:377
  129.7 5.2 %collective-permute-start.20 = (bf16[8,768]{1,0:T(8,128)(2,1)S(1)}, bf16[8,768]{1,0:T(8,128)(2,1)S(1)}, u32[]{:S(2)}, u32[]{:S(2)}) collective-permute-start(bf16[8,768]{1,0:T(8,128)(2,1)S(1)} %max.16), channel_id=1, source_target_pairs={{0,4},{1,5},{2,6},{3,7},{4,0},{5,1},{6,2},{7,3},{8,12},{9,13},{10,... | collective-permute-start | bytes 36872 | tf_op jit(solution)/shard_map/ppermute | solution.py:377
  129.7 5.2 %collective-permute-start.19 = (bf16[8,768]{1,0:T(8,128)(2,1)S(1)}, bf16[8,768]{1,0:T(8,128)(2,1)S(1)}, u32[]{:S(2)}, u32[]{:S(2)}) collective-permute-start(bf16[8,768]{1,0:T(8,128)(2,1)S(1)} %max.16), channel_id=1, source_target_pairs={{0,2},{1,3},{2,0},{3,1},{4,6},{5,7},{6,4},{7,5},{8,10},{9,11},{10,... | collective-permute-start | bytes 36872 | tf_op jit(solution)/shard_map/ppermute | solution.py:377
  (13 other events, 12.5 us)

commit v2 on v1

--- a/solution.py
+++ b/solution.py
@@ -1,4 +1,5 @@
 import functools
+import itertools
 
 import jax
 import jax.numpy as jnp
@@ -18,6 +19,7 @@
 WHOLE = (False, True)
 SIDE = 4
 STEP = 2
+ENDSTEP = 4
 PLACES = 8
 
 
@@ -219,25 +221,25 @@
         query_ref, key_ref, value_ref = outs[-3:]
     else:
         query_ref, key_ref, value_ref, peak_ref = outs[-4:]
-    _, rows, _ = moved_refs[0].shape
+    count, rows, _ = moved_refs[0].shape
     piece = rows // SLOTS
     dim = PLACES * piece
-    for s in range(SLOTS):
-        held = jnp.concatenate([ref[0, s * piece : (s + 1) * piece, :] for ref in moved_refs], axis=0)
+    for n, s in itertools.product(range(count), range(SLOTS)):
+        held = jnp.concatenate([ref[n, s * piece : (s + 1) * piece, :] for ref in moved_refs], axis=0)
         turned = jnp.dot(turn_ref[s // (SLOTS - 1)], held, preferred_element_type=jnp.float32)
         if gain_ref is not None:
-            turned = turned * gain_ref[pl.ds(first + pl.program_id(0), 1), :]
+            turned = turned * gain_ref[pl.ds(first + pl.program_id(0) * count + n, 1), :]
         turned = turned.astype(jnp.bfloat16)
         if s < GROUP:
-            query_ref[0, s * dim : (s + 1) * dim, :] = turned
+            query_ref[n, s * dim : (s + 1) * dim, :] = turned
         elif s == GROUP:
-            key_ref[0] = turned
+            key_ref[n] = turned
         else:
-            value_ref[0] = turned
+            value_ref[n] = turned
         if gain_ref is not None:
             size = jnp.abs(turned.astype(jnp.float32))
             size = jnp.maximum(size[:, :128], size[:, 128:])
-            peak_ref[0, :, s * dim : (s + 1) * dim] = jnp.max(size.T, axis=0, keepdims=True)
+            peak_ref[n, :, s * dim : (s + 1) * dim] = jnp.max(size.T, axis=0, keepdims=True)
 
 
 def plain_body(turn_ref, *refs):
@@ -253,7 +255,7 @@
     dim = turn.shape[1]
 
     def at(*shape):
-        return pl.BlockSpec((1, *shape), lambda l: (first + l, 0, 0))
+        return pl.BlockSpec((ENDSTEP, *shape), lambda l: (first // ENDSTEP + l, 0, 0))
 
     shapes = [
         ((GROUP * dim, width), jnp.bfloat16),
@@ -269,15 +271,15 @@
         body = functools.partial(scaled_body, first)
         before.append(gain)
         in_specs.append(pl.BlockSpec(gain.shape, lambda l: (0, 0)))
-        out_specs.append(pl.BlockSpec((1, 1, SLOTS * dim), lambda l: (l, 0, 0)))
+        out_specs.append(pl.BlockSpec((ENDSTEP, 1, SLOTS * dim), lambda l: (l, 0, 0)))
         out_shape.append(jax.ShapeDtypeStruct((layers, 1, SLOTS * dim), jnp.float32))
     if len(moved) == 1:
         held = [
-            pl.BlockSpec((None, 1, rows, width), lambda l, k=k: (k, l, 0, 0)) for k in range(PLACES)
+            pl.BlockSpec((None, ENDSTEP, rows, width), lambda l, k=k: (k, l, 0, 0)) for k in range(PLACES)
         ]
         moved = moved * PLACES
     else:
-        held = [pl.BlockSpec((1, rows, width), lambda l: (l, 0, 0))] * PLACES
+        held = [pl.BlockSpec((ENDSTEP, rows, width), lambda l: (l, 0, 0))] * PLACES
     shapes = [
         ((GROUP * dim, width), jnp.bfloat16),
         ((dim, width), jnp.bfloat16),
@@ -285,7 +287,7 @@
     ]
     return pl.pallas_call(
         body,
-        grid=(layers,),
+        grid=(layers // ENDSTEP,),
         in_specs=in_specs + held + [pl.BlockSpec(memory_space=pltpu.HBM)] * len(earlier),
         out_specs=out_specs,
         out_shape=out_shape,
@@ -328,7 +330,7 @@
 
 STAGE = ((2, 1), (1, 1), (3, 1), (0, 1), (2, 0), (1, 0), (3, 0))
 
-LAST = ((2, 1), (1, 0), (2, 0), (0, 1), (3, 1), (3, 0), (1, 1))
+LAST = ((3, 1), (1, 0), (2, 1), (2, 0), (0, 1), (3, 0), (1, 1))
 
 
 def staged(buffers, move, order):
@@ -388,7 +390,7 @@
     return query, key, value, row_peak
 
 
-JOINS = ((1,), (8,), (2, 4, 6))
+JOINS = ((1,), (2, 4, 6), (8,))
 
 
 def solution(mesh):

time: 142 us -> 140 us (0.986)
  the two profiles are of different devices: /device:TPU:2 before, /device:TPU:0 now
where the time goes in v2:
time: 140 us
  waiting for transfers between devices  61.7 us (44%)
  starting transfers between devices  46.6 us (33%)
  Pallas kernels  19 us (14%)
  local copies, waits for them, and re-layouts  8.4 us (6%)
  other arithmetic  3.02 us (2%)
    ppermute x7, waiting for transfers between devices, first_move(): return lax.ppermute(array, ('dev', 'ma'), pairs)  25.1 us
    ppermute x5, waiting for transfers between devices, shards(): lax.ppermute(peak, 'ma', [(j, j ^ step) for j in range(16)])  21.8 us
    all_to_all x2, starting transfers between devices, exchange(): lax.all_to_all(array, ('dev', 'ma'), 0, 0, tiled=True, axis_index_groups=...  19.8 us
    ppermute x7, waiting for transfers between devices, second_move(): return lax.ppermute(array, ('dev', 'ma'), pairs)  14.3 us
    ppermute x7, starting transfers between devices, first_move(): return lax.ppermute(array, ('dev', 'ma'), pairs)  12.6 us
    pallas_call x2, Pallas kernels, prepare(): pl.pallas_call(functools.partial(prepare_body, first), grid_spec=pltpu.Pr...  8.12 us
    ppermute x7, starting transfers between devices, second_move(): return lax.ppermute(array, ('dev', 'ma'), pairs)  7.11 us
    pallas_call x2, Pallas kernels, finish(): pl.pallas_call(body, grid=(layers // ENDSTEP,), in_specs=in_specs + held...  6.35 us
  transfers between devices with their start and end apart: 24, of which 12 were waited for; matrix products, arithmetic and copies ran while one was open for 2% of the time, Pallas kernels for 10%

profile of v2, /device:TPU:0, one launch (start us, length us, event | category | flops | bytes accessed | tf_op | source)
XLA Modules:
  0.0 139.9 jit_solution(2281565697977642303)
XLA Ops:
  0.7 1.6 %constant_dynamic-slice_fusion = (bf16[4,256,384]{2,1,0:T(8,128)(2,1)S(1)}, bf16[4,256,384]{2,1,0:T(8,128)(2,1)S(1)}) fusion(bf16[8,512,384]{2,1,0:T(8,128)(2,1)} %own_ref.3, s32[]{:T(128)S(6)} %select_n.44), kind=kLoop, calls=%fused_computation.33 | loop fusion | bytes 3145732 | tf_op jit(solution)/shard_map/dynamic_slice | solution.py:355
  5.6 4.1 %prepare.2 = bf16[8,4,96,256]{3,2,1,0:T(8,128)(2,1)} custom-call(s32[3]{0:T(128)} %pad_add_fusion.1.place_ref, bf16[384,384]{1,0:T(8,128)(2,1)} %constant.73.clone.pick_ref, f32[8,256]{1,0:T(8,128)} %copy-done.19, bf16[8,512,384]{2,1,0:T(8,128)(2,1)} %own_ref.3, bf16[4,256,384]{2,1,0:T(8,128)(2,1)} %copy-done.3), custom_call_target="tpu_custom_call" | custom-call | tf_op jit(solution)/shard_map/prepare/pallas_call | solution.py:114
  9.6 16.2 %all-to-all-start = ((bf16[8,4,96,256]{3,2,1,0:T(8,128)(2,1)}), bf16[8,4,96,256]{3,2,1,0:T(8,128)(2,1)S(1)}, u32[]{:S(2)}, u32[]{:S(2)}) async-start(bf16[8,4,96,256]{3,2,1,0:T(8,128)(2,1)} %prepare.2), calls=%async_computation | async-start | bytes 3145728 | tf_op jit(solution)/shard_map/all_to_all | solution.py:328
  26.8 4.0 %prepare.3 = (bf16[4,96,256]{2,1,0:T(8,128)(2,1)}, bf16[4,96,256]{2,1,0:T(8,128)(2,1)}, bf16[4,96,256]{2,1,0:T(8,128)(2,1)}, bf16[4,96,256]{2,1,0:T(8,128)(2,1)}...) custom-call(s32[3]{0:T(128)} %pad_add_fusion.1.place_ref, ...), custom_call_target="tpu_custom_call" | custom-call | tf_op jit(solution)/shard_map/prepare/pallas_call | solution.py:114
  30.8 2.1 %collective-permute-start.3 = (bf16[4,96,256]{2,1,0:T(8,128)(2,1)}, bf16[4,96,256]{2,1,0:T(8,128)(2,1)S(1)}, u32[]{:S(2)}, u32[]{:S(2)}) collective-permute-start(bf16[4,96,256]{2,1,0:T(8,128)(2,1)} %get-tuple-element.28), channel_id=1, source_target_pairs={{0,16},{1,17},{2,18},{3,19},{4,20},{5,21},{6,22},{7,23},{8,24},{9,... | collective-permute-start | bytes 589832 | tf_op jit(solution)/shard_map/ppermute | solution.py:48
  32.9 2.7 %collective-permute-start.4 = (bf16[4,96,256]{2,1,0:T(8,128)(2,1)}, bf16[4,96,256]{2,1,0:T(8,128)(2,1)S(1)}, u32[]{:S(2)}, u32[]{:S(2)}) collective-permute-start(bf16[4,96,256]{2,1,0:T(8,128)(2,1)} %get-tuple-element.29), channel_id=1, source_target_pairs={{0,32},{1,33},{2,34},{3,35},{4,36},{5,37},{6,38},{7,39},{8,40},{9,... | collective-permute-start | bytes 589832 | tf_op jit(solution)/shard_map/ppermute | solution.py:48
  35.6 1.5 %collective-permute-start.5 = (bf16[4,96,256]{2,1,0:T(8,128)(2,1)}, bf16[4,96,256]{2,1,0:T(8,128)(2,1)S(1)}, u32[]{:S(2)}, u32[]{:S(2)}) collective-permute-start(bf16[4,96,256]{2,1,0:T(8,128)(2,1)} %get-tuple-element.30), channel_id=1, source_target_pairs={{0,48},{1,49},{2,50},{3,51},{4,52},{5,53},{6,54},{7,55},{8,56},{9,... | collective-permute-start | bytes 589832 | tf_op jit(solution)/shard_map/ppermute | solution.py:48
  37.1 2.7 %collective-permute-start.6 = (bf16[4,96,256]{2,1,0:T(8,128)(2,1)}, bf16[4,96,256]{2,1,0:T(8,128)(2,1)S(1)}, u32[]{:S(2)}, u32[]{:S(2)}) collective-permute-start(bf16[4,96,256]{2,1,0:T(8,128)(2,1)} %get-tuple-element.31), channel_id=1, source_target_pairs={{0,72},{1,73},{2,74},{3,75},{4,76},{5,77},{6,78},{7,79},{8,64},{9,... | collective-permute-start | bytes 589832 | tf_op jit(solution)/shard_map/ppermute | solution.py:48
  40.4 11.8 %collective-permute-done.3.refs_1_ = bf16[4,96,256]{2,1,0:T(8,128)(2,1)S(1)} collective-permute-done((bf16[4,96,256]{2,1,0:T(8,128)(2,1)}, bf16[4,96,256]{2,1,0:T(8,128)(2,1)S(1)}, u32[]{:S(2)}, u32[]{:S(2)}) %collective-permute-start.3) | collective-permute-done | bytes 196640 | tf_op jit(solution)/shard_map/ppermute | solution.py:48
  52.2 3.1 %collective-permute-start.8 = (bf16[4,96,256]{2,1,0:T(8,128)(2,1)}, bf16[4,96,256]{2,1,0:T(8,128)(2,1)S(1)}, u32[]{:S(2)}, u32[]{:S(2)}) collective-permute-start(bf16[4,96,256]{2,1,0:T(8,128)(2,1)} %get-tuple-element.33), channel_id=1, source_target_pairs={{0,104},{1,105},{2,106},{3,107},{4,108},{5,109},{6,110},{7,111},{8... | collective-permute-start | bytes 589832 | tf_op jit(solution)/shard_map/ppermute | solution.py:48
  55.2 1.1 collective-permute-done.4.refs_2_
  56.5 11.3 %collective-permute-done.7.refs_5_ = bf16[4,96,256]{2,1,0:T(8,128)(2,1)S(1)} collective-permute-done((bf16[4,96,256]{2,1,0:T(8,128)(2,1)}, bf16[4,96,256]{2,1,0:T(8,128)(2,1)S(1)}, u32[]{:S(2)}, u32[]{:S(2)}) %collective-permute-start.7) | collective-permute-done | bytes 196640 | tf_op jit(solution)/shard_map/ppermute | solution.py:48
  69.3 2.3 %reorder.1 = (bf16[4,96,256]{2,1,0:T(8,128)(2,1)}, bf16[4,96,256]{2,1,0:T(8,128)(2,1)}, bf16[4,96,256]{2,1,0:T(8,128)(2,1)}, bf16[4,96,256]{2,1,0:T(8,128)(2,1)}...) custom-call(bf16[4,96,256]{2,1,0:T(8,128)(2,1)} %get-tuple-element.2, ...), custom_call_target="tpu_custom_call" | custom-call | tf_op jit(solution)/shard_map/reorder/pallas_call | solution.py:161
  71.6 1.4 collective-permute-start.10
  73.0 1.3 collective-permute-start.11
  75.0 1.5 %collective-permute-start.12 = (bf16[4,96,256]{2,1,0:T(8,128)(2,1)}, bf16[4,96,256]{2,1,0:T(8,128)(2,1)S(1)}, u32[]{:S(2)}, u32[]{:S(2)}) collective-permute-start(bf16[4,96,256]{2,1,0:T(8,128)(2,1)} %get-tuple-element.38), channel_id=1, source_target_pairs={{0,6},{1,7},{2,0},{3,1},{4,2},{5,3},{6,4},{7,5},{8,14},{9,15},{10,... | collective-permute-start | bytes 589832 | tf_op jit(solution)/shard_map/ppermute | solution.py:53
  76.5 2.0 %collective-permute-start.14 = (bf16[4,96,256]{2,1,0:T(8,128)(2,1)}, bf16[4,96,256]{2,1,0:T(8,128)(2,1)S(1)}, u32[]{:S(2)}, u32[]{:S(2)}) collective-permute-start(bf16[4,96,256]{2,1,0:T(8,128)(2,1)} %get-tuple-element.40), channel_id=1, source_target_pairs={{0,10},{1,11},{2,12},{3,13},{4,14},{5,15},{6,8},{7,9},{8,2},{9,3},... | collective-permute-start | bytes 589832 | tf_op jit(solution)/shard_map/ppermute | solution.py:53
  78.5 1.8 %collective-permute-done.10.refs_1_ = bf16[4,96,256]{2,1,0:T(8,128)(2,1)S(1)} collective-permute-done((bf16[4,96,256]{2,1,0:T(8,128)(2,1)}, bf16[4,96,256]{2,1,0:T(8,128)(2,1)S(1)}, u32[]{:S(2)}, u32[]{:S(2)}) %collective-permute-start.10) | collective-permute-done | bytes 196640 | tf_op jit(solution)/shard_map/ppermute | solution.py:53
  80.3 3.2 %collective-permute-done.11.refs_2_ = bf16[4,96,256]{2,1,0:T(8,128)(2,1)S(1)} collective-permute-done((bf16[4,96,256]{2,1,0:T(8,128)(2,1)}, bf16[4,96,256]{2,1,0:T(8,128)(2,1)S(1)}, u32[]{:S(2)}, u32[]{:S(2)}) %collective-permute-start.11) | collective-permute-done | bytes 196640 | tf_op jit(solution)/shard_map/ppermute | solution.py:53
  83.6 0.9 collective-permute-start.16
  85.5 8.4 %collective-permute-done.13.refs_4_ = bf16[4,96,256]{2,1,0:T(8,128)(2,1)S(1)} collective-permute-done((bf16[4,96,256]{2,1,0:T(8,128)(2,1)}, bf16[4,96,256]{2,1,0:T(8,128)(2,1)S(1)}, u32[]{:S(2)}, u32[]{:S(2)}) %collective-permute-start.13) | collective-permute-done | bytes 196640 | tf_op jit(solution)/shard_map/ppermute | solution.py:53
  94.8 3.2 %finish.2 = (bf16[8,512,256]{2,1,0:T(8,128)(2,1)}, bf16[8,128,256]{2,1,0:T(8,128)(2,1)}, bf16[8,128,256]{2,1,0:T(8,128)(2,1)}, f32[4,1,768]{2,1,0:T(1,128)}) custom-call(bf16[2,128,128]{2,1,0:T(8,128)(2,1)} %get-tuple-element.54.turn_ref, f32[8,256]{1,0:T(8,128)} %gain_ref.3, bf16[4,96,256]{2,1,0:T(8,128)(2,1)} %get-tuple-element.35.refs_0_, ...), custom_call_target="tpu_custom_call" | custom-call | tf_op jit(solution)/shard_map/finish/pallas_call | solution.py:288
  98.8 1.2 copy-done
  99.9 2.3 %peaks.1 = f32[2,384]{1,0:T(2,128)} custom-call(bf16[8,4,96,256]{3,2,1,0:T(8,128)(2,1)} %copy-done, bf16[8,4,96,256]{3,2,1,0:T(8,128)(2,1)} %copy-done, bf16[8,4,96,256]{3,2,1,0:T(8,128)(2,1)} %copy-done, bf16[8,4,96,256]{3,2,1,0:T(8,128)(2,1)} %copy-done, bf16[8,4,96,256]{3,2,1,0:T(8,128)(2,1)} %copy-done, bf16[8,4,96,256]{3,2,1,0:T(8,128)(2,1)} %copy-done, ...), custom_call_target="tpu_custom_call" | custom-call | tf_op jit(solution)/shard_map/peaks/pallas_call | solution.py:196
  103.6 3.6 %all-to-all-start.1 = ((bf16[8,4,96,256]{3,2,1,0:T(8,128)(2,1)}), bf16[8,4,96,256]{3,2,1,0:T(8,128)(2,1)S(1)}, u32[]{:S(2)}, u32[]{:S(2)}) async-start(bf16[8,4,96,256]{3,2,1,0:T(8,128)(2,1)} %copy-done), calls=%async_computation.1 | async-start | bytes 3145728 | tf_op jit(solution)/shard_map/all_to_all | solution.py:328
  107.2 3.2 %collective-permute-start.20 = (bf16[8,768]{1,0:T(8,128)(2,1)S(1)}, bf16[8,768]{1,0:T(8,128)(2,1)S(1)}, u32[]{:S(2)}, u32[]{:S(2)}) collective-permute-start(bf16[8,768]{1,0:T(8,128)(2,1)S(1)} %fusion.8), channel_id=1, source_target_pairs={{0,6},{1,7},{2,4},{3,5},{4,2},{5,3},{6,0},{7,1},{8,14},{9,15},{10,... | collective-permute-start | bytes 36872 | tf_op jit(solution)/shard_map/ppermute | solution.py:379
  111.4 17.3 %collective-permute-done.20 = bf16[8,768]{1,0:T(8,128)(2,1)S(1)} collective-permute-done((bf16[8,768]{1,0:T(8,128)(2,1)S(1)}, bf16[8,768]{1,0:T(8,128)(2,1)S(1)}, u32[]{:S(2)}, u32[]{:S(2)}) %collective-permute-start.20) | collective-permute-done | bytes 12320 | tf_op jit(solution)/shard_map/ppermute | solution.py:379
  128.7 2.2 %collective-permute-done.19 = bf16[8,768]{1,0:T(8,128)(2,1)S(1)} collective-permute-done((bf16[8,768]{1,0:T(8,128)(2,1)S(1)}, bf16[8,768]{1,0:T(8,128)(2,1)S(1)}, u32[]{:S(2)}, u32[]{:S(2)}) %collective-permute-start.19) | collective-permute-done | bytes 12320 | tf_op jit(solution)/shard_map/ppermute | solution.py:379
  131.0 1.6 %collective-permute-start.21 = (bf16[8,768]{1,0:T(8,128)(2,1)S(1)}, bf16[8,768]{1,0:T(8,128)(2,1)S(1)}, u32[]{:S(2)}, u32[]{:S(2)}) collective-permute-start(bf16[8,768]{1,0:T(8,128)(2,1)S(1)} %maximum_maximum_fusion), channel_id=1, source_target_pairs={{0,8},{1,9},{2,10},{3,11},{4,12},{5,13},{6,14},{7,15},{8,0},{9,1},... | collective-permute-start | bytes 36872 | tf_op jit(solution)/shard_map/ppermute | solution.py:379
  132.5 2.2 %collective-permute-done.21 = bf16[8,768]{1,0:T(8,128)(2,1)S(1)} collective-permute-done((bf16[8,768]{1,0:T(8,128)(2,1)S(1)}, bf16[8,768]{1,0:T(8,128)(2,1)S(1)}, u32[]{:S(2)}, u32[]{:S(2)}) %collective-permute-start.21) | collective-permute-done | bytes 12320 | tf_op jit(solution)/shard_map/ppermute | solution.py:379
  135.6 1.2 copy-done.1
  136.7 3.1 %finish.3 = (bf16[8,512,256]{2,1,0:T(8,128)(2,1)}, bf16[8,128,256]{2,1,0:T(8,128)(2,1)}, bf16[8,128,256]{2,1,0:T(8,128)(2,1)}) custom-call(bf16[2,128,128]{2,1,0:T(8,128)(2,1)} %get-tuple-element.55.turn_ref, bf16[8,4,96,256]{3,2,1,0:T(8,128)(2,1)} %copy-done.1, ...), custom_call_target="tpu_custom_call", output_to_operand_aliasing={{0}: (9, {}), {1}: (10, {}), {2}: (11, {})} | custom-call | tf_op jit(solution)/shard_map/finish/pallas_call | solution.py:288
  (92 shorter events, 12.8 us)
Async XLA Ops:
  2.2 2.4 %collective-permute-start.1 = (bf16[4,256,384]{2,1,0:T(8,128)(2,1)S(1)}, bf16[4,256,384]{2,1,0:T(8,128)(2,1)S(1)}, u32[]{:S(2)}, u32[]{:S(2)}) collective-permute-start(bf16[4,256,384]{2,1,0:T(8,128)(2,1)S(1)} %get-tuple-element.51), channel_id=1, source_target_pairs={{0,1},{1,0},{2,3},{3,2},{4,5},{5,4},{6,7},{7,6},{8,9},{9,8},{10,11... | collective-permute-start | bytes 2359304 | tf_op jit(solution)/shard_map/ppermute | solution.py:38
  2.3 23.6 %collective-permute-start.2 = (bf16[4,256,384]{2,1,0:T(8,128)(2,1)S(1)}, bf16[4,256,384]{2,1,0:T(8,128)(2,1)S(1)}, u32[]{:S(2)}, u32[]{:S(2)}) collective-permute-start(bf16[4,256,384]{2,1,0:T(8,128)(2,1)S(1)} %get-tuple-element.50), channel_id=1, source_target_pairs={{0,1},{1,0},{2,3},{3,2},{4,5},{5,4},{6,7},{7,6},{8,9},{9,8},{10,11... | collective-permute-start | bytes 2359304 | tf_op jit(solution)/shard_map/ppermute | solution.py:38
  2.8 1.3 collective-permute-start
  9.6 89.1 %all-to-all-start = ((bf16[8,4,96,256]{3,2,1,0:T(8,128)(2,1)}), bf16[8,4,96,256]{3,2,1,0:T(8,128)(2,1)S(1)}, u32[]{:S(2)}, u32[]{:S(2)}) async-start(bf16[8,4,96,256]{3,2,1,0:T(8,128)(2,1)} %prepare.2), calls=%async_computation | async-start | bytes 3145728 | tf_op jit(solution)/shard_map/all_to_all | solution.py:328
  25.9 30.5 %copy-start.20 = (s32[128]{0:T(128)S(1)}, s32[128]{0:T(128)}, u32[]{:S(2)}) copy-start(s32[128]{0:T(128)} %param.7) | copy-start | bytes 1540
  30.8 21.3 %collective-permute-start.3 = (bf16[4,96,256]{2,1,0:T(8,128)(2,1)}, bf16[4,96,256]{2,1,0:T(8,128)(2,1)S(1)}, u32[]{:S(2)}, u32[]{:S(2)}) collective-permute-start(bf16[4,96,256]{2,1,0:T(8,128)(2,1)} %get-tuple-element.28), channel_id=1, source_target_pairs={{0,16},{1,17},{2,18},{3,19},{4,20},{5,21},{6,22},{7,23},{8,24},{9,... | collective-permute-start | bytes 589832 | tf_op jit(solution)/shard_map/ppermute | solution.py:48
  32.9 23.5 %collective-permute-start.4 = (bf16[4,96,256]{2,1,0:T(8,128)(2,1)}, bf16[4,96,256]{2,1,0:T(8,128)(2,1)S(1)}, u32[]{:S(2)}, u32[]{:S(2)}) collective-permute-start(bf16[4,96,256]{2,1,0:T(8,128)(2,1)} %get-tuple-element.29), channel_id=1, source_target_pairs={{0,32},{1,33},{2,34},{3,35},{4,36},{5,37},{6,38},{7,39},{8,40},{9,... | collective-permute-start | bytes 589832 | tf_op jit(solution)/shard_map/ppermute | solution.py:48
  35.6 20.8 %collective-permute-start.5 = (bf16[4,96,256]{2,1,0:T(8,128)(2,1)}, bf16[4,96,256]{2,1,0:T(8,128)(2,1)S(1)}, u32[]{:S(2)}, u32[]{:S(2)}) collective-permute-start(bf16[4,96,256]{2,1,0:T(8,128)(2,1)} %get-tuple-element.30), channel_id=1, source_target_pairs={{0,48},{1,49},{2,50},{3,51},{4,52},{5,53},{6,54},{7,55},{8,56},{9,... | collective-permute-start | bytes 589832 | tf_op jit(solution)/shard_map/ppermute | solution.py:48
  37.1 19.3 %collective-permute-start.6 = (bf16[4,96,256]{2,1,0:T(8,128)(2,1)}, bf16[4,96,256]{2,1,0:T(8,128)(2,1)S(1)}, u32[]{:S(2)}, u32[]{:S(2)}) collective-permute-start(bf16[4,96,256]{2,1,0:T(8,128)(2,1)} %get-tuple-element.31), channel_id=1, source_target_pairs={{0,72},{1,73},{2,74},{3,75},{4,76},{5,77},{6,78},{7,79},{8,64},{9,... | collective-permute-start | bytes 589832 | tf_op jit(solution)/shard_map/ppermute | solution.py:48
  39.8 28.0 %collective-permute-start.7 = (bf16[4,96,256]{2,1,0:T(8,128)(2,1)}, bf16[4,96,256]{2,1,0:T(8,128)(2,1)S(1)}, u32[]{:S(2)}, u32[]{:S(2)}) collective-permute-start(bf16[4,96,256]{2,1,0:T(8,128)(2,1)} %get-tuple-element.32), channel_id=1, source_target_pairs={{0,88},{1,89},{2,90},{3,91},{4,92},{5,93},{6,94},{7,95},{8,80},{9,... | collective-permute-start | bytes 589832 | tf_op jit(solution)/shard_map/ppermute | solution.py:48
  52.2 16.5 %copy-start.4 = (bf16[4,96,256]{2,1,0:T(8,128)(2,1)}, bf16[4,96,256]{2,1,0:T(8,128)(2,1)S(1)}, u32[]{:S(2)}) copy-start(bf16[4,96,256]{2,1,0:T(8,128)(2,1)S(1)} %collective-permute-done.3.refs_1_) | copy-start | bytes 589828
  52.2 15.6 %collective-permute-start.8 = (bf16[4,96,256]{2,1,0:T(8,128)(2,1)}, bf16[4,96,256]{2,1,0:T(8,128)(2,1)S(1)}, u32[]{:S(2)}, u32[]{:S(2)}) collective-permute-start(bf16[4,96,256]{2,1,0:T(8,128)(2,1)} %get-tuple-element.33), channel_id=1, source_target_pairs={{0,104},{1,105},{2,106},{3,107},{4,108},{5,109},{6,110},{7,111},{8... | collective-permute-start | bytes 589832 | tf_op jit(solution)/shard_map/ppermute | solution.py:48
  56.4 12.3 %copy-start.5 = (bf16[4,96,256]{2,1,0:T(8,128)(2,1)}, bf16[4,96,256]{2,1,0:T(8,128)(2,1)S(1)}, u32[]{:S(2)}) copy-start(bf16[4,96,256]{2,1,0:T(8,128)(2,1)S(1)} %collective-permute-done.4.refs_2_) | copy-start | bytes 589828
  56.4 12.2 %collective-permute-start.9 = (bf16[4,96,256]{2,1,0:T(8,128)(2,1)}, bf16[4,96,256]{2,1,0:T(8,128)(2,1)S(1)}, u32[]{:S(2)}, u32[]{:S(2)}) collective-permute-start(bf16[4,96,256]{2,1,0:T(8,128)(2,1)} %get-tuple-element.34), channel_id=1, source_target_pairs={{0,120},{1,121},{2,122},{3,123},{4,124},{5,125},{6,126},{7,127},{8... | collective-permute-start | bytes 589832 | tf_op jit(solution)/shard_map/ppermute | solution.py:48
  56.4 12.2 %copy-start.7 = (bf16[4,96,256]{2,1,0:T(8,128)(2,1)}, bf16[4,96,256]{2,1,0:T(8,128)(2,1)S(1)}, u32[]{:S(2)}) copy-start(bf16[4,96,256]{2,1,0:T(8,128)(2,1)S(1)} %collective-permute-done.5.refs_3_) | copy-start | bytes 589828
  56.5 12.2 %copy-start.9 = (bf16[4,96,256]{2,1,0:T(8,128)(2,1)}, bf16[4,96,256]{2,1,0:T(8,128)(2,1)S(1)}, u32[]{:S(2)}) copy-start(bf16[4,96,256]{2,1,0:T(8,128)(2,1)S(1)} %collective-permute-done.6.refs_4_) | copy-start | bytes 589828
  71.6 8.7 %collective-permute-start.10 = (bf16[4,96,256]{2,1,0:T(8,128)(2,1)}, bf16[4,96,256]{2,1,0:T(8,128)(2,1)S(1)}, u32[]{:S(2)}, u32[]{:S(2)}) collective-permute-start(bf16[4,96,256]{2,1,0:T(8,128)(2,1)} %get-tuple-element.36), channel_id=1, source_target_pairs={{0,2},{1,3},{2,4},{3,5},{4,6},{5,7},{6,0},{7,1},{8,10},{9,11},{10,... | collective-permute-start | bytes 589832 | tf_op jit(solution)/shard_map/ppermute | solution.py:53
  73.0 10.6 %collective-permute-start.11 = (bf16[4,96,256]{2,1,0:T(8,128)(2,1)}, bf16[4,96,256]{2,1,0:T(8,128)(2,1)S(1)}, u32[]{:S(2)}, u32[]{:S(2)}) collective-permute-start(bf16[4,96,256]{2,1,0:T(8,128)(2,1)} %get-tuple-element.37), channel_id=1, source_target_pairs={{0,4},{1,5},{2,6},{3,7},{4,0},{5,1},{6,2},{7,3},{8,12},{9,13},{10,... | collective-permute-start | bytes 589832 | tf_op jit(solution)/shard_map/ppermute | solution.py:53
  75.0 10.4 %collective-permute-start.12 = (bf16[4,96,256]{2,1,0:T(8,128)(2,1)}, bf16[4,96,256]{2,1,0:T(8,128)(2,1)S(1)}, u32[]{:S(2)}, u32[]{:S(2)}) collective-permute-start(bf16[4,96,256]{2,1,0:T(8,128)(2,1)} %get-tuple-element.38), channel_id=1, source_target_pairs={{0,6},{1,7},{2,0},{3,1},{4,2},{5,3},{6,4},{7,5},{8,14},{9,15},{10,... | collective-permute-start | bytes 589832 | tf_op jit(solution)/shard_map/ppermute | solution.py:53
  76.5 17.4 %collective-permute-start.13 = (bf16[4,96,256]{2,1,0:T(8,128)(2,1)}, bf16[4,96,256]{2,1,0:T(8,128)(2,1)S(1)}, u32[]{:S(2)}, u32[]{:S(2)}) collective-permute-start(bf16[4,96,256]{2,1,0:T(8,128)(2,1)} %get-tuple-element.39), channel_id=1, source_target_pairs={{0,8},{1,9},{2,10},{3,11},{4,12},{5,13},{6,14},{7,15},{8,0},{9,1},... | collective-permute-start | bytes 589832 | tf_op jit(solution)/shard_map/ppermute | solution.py:53
  76.5 17.4 %collective-permute-start.14 = (bf16[4,96,256]{2,1,0:T(8,128)(2,1)}, bf16[4,96,256]{2,1,0:T(8,128)(2,1)S(1)}, u32[]{:S(2)}, u32[]{:S(2)}) collective-permute-start(bf16[4,96,256]{2,1,0:T(8,128)(2,1)} %get-tuple-element.40), channel_id=1, source_target_pairs={{0,10},{1,11},{2,12},{3,13},{4,14},{5,15},{6,8},{7,9},{8,2},{9,3},... | collective-permute-start | bytes 589832 | tf_op jit(solution)/shard_map/ppermute | solution.py:53
  80.3 13.6 %copy-start.6 = (bf16[4,96,256]{2,1,0:T(8,128)(2,1)}, bf16[4,96,256]{2,1,0:T(8,128)(2,1)S(1)}, u32[]{:S(2)}) copy-start(bf16[4,96,256]{2,1,0:T(8,128)(2,1)S(1)} %collective-permute-done.10.refs_1_) | copy-start | bytes 589828
  80.3 13.6 %collective-permute-start.15 = (bf16[4,96,256]{2,1,0:T(8,128)(2,1)}, bf16[4,96,256]{2,1,0:T(8,128)(2,1)S(1)}, u32[]{:S(2)}, u32[]{:S(2)}) collective-permute-start(bf16[4,96,256]{2,1,0:T(8,128)(2,1)} %get-tuple-element.41), channel_id=1, source_target_pairs={{0,12},{1,13},{2,14},{3,15},{4,8},{5,9},{6,10},{7,11},{8,4},{9,5},... | collective-permute-start | bytes 589832 | tf_op jit(solution)/shard_map/ppermute | solution.py:53
  83.6 10.4 %copy-start.8 = (bf16[4,96,256]{2,1,0:T(8,128)(2,1)}, bf16[4,96,256]{2,1,0:T(8,128)(2,1)S(1)}, u32[]{:S(2)}) copy-start(bf16[4,96,256]{2,1,0:T(8,128)(2,1)S(1)} %collective-permute-done.11.refs_2_) | copy-start | bytes 589828
  83.6 10.3 %collective-permute-start.16 = (bf16[4,96,256]{2,1,0:T(8,128)(2,1)}, bf16[4,96,256]{2,1,0:T(8,128)(2,1)S(1)}, u32[]{:S(2)}, u32[]{:S(2)}) collective-permute-start(bf16[4,96,256]{2,1,0:T(8,128)(2,1)} %get-tuple-element.42), channel_id=1, source_target_pairs={{0,14},{1,15},{2,8},{3,9},{4,10},{5,11},{6,12},{7,13},{8,6},{9,7},... | collective-permute-start | bytes 589832 | tf_op jit(solution)/shard_map/ppermute | solution.py:53
  85.5 8.5 %copy-start.11 = (bf16[4,96,256]{2,1,0:T(8,128)(2,1)}, bf16[4,96,256]{2,1,0:T(8,128)(2,1)S(1)}, u32[]{:S(2)}) copy-start(bf16[4,96,256]{2,1,0:T(8,128)(2,1)S(1)} %collective-permute-done.12.refs_3_) | copy-start | bytes 589828
  103.5 3.7 %collective-permute-start.17 = (bf16[8,768]{1,0:T(8,128)(2,1)S(1)}, bf16[8,768]{1,0:T(8,128)(2,1)S(1)}, u32[]{:S(2)}, u32[]{:S(2)}) collective-permute-start(bf16[8,768]{1,0:T(8,128)(2,1)S(1)} %pad_maximum_fusion.1), channel_id=1, source_target_pairs={{0,1},{1,0},{2,3},{3,2},{4,5},{5,4},{6,7},{7,6},{8,9},{9,8},{10,11... | collective-permute-start | bytes 36872 | tf_op jit(solution)/shard_map/ppermute | solution.py:379
  103.6 32.0 %all-to-all-start.1 = ((bf16[8,4,96,256]{3,2,1,0:T(8,128)(2,1)}), bf16[8,4,96,256]{3,2,1,0:T(8,128)(2,1)S(1)}, u32[]{:S(2)}, u32[]{:S(2)}) async-start(bf16[8,4,96,256]{3,2,1,0:T(8,128)(2,1)} %copy-done), calls=%async_computation.1 | async-start | bytes 3145728 | tf_op jit(solution)/shard_map/all_to_all | solution.py:328
  107.2 21.5 %collective-permute-start.20 = (bf16[8,768]{1,0:T(8,128)(2,1)S(1)}, bf16[8,768]{1,0:T(8,128)(2,1)S(1)}, u32[]{:S(2)}, u32[]{:S(2)}) collective-permute-start(bf16[8,768]{1,0:T(8,128)(2,1)S(1)} %fusion.8), channel_id=1, source_target_pairs={{0,6},{1,7},{2,4},{3,5},{4,2},{5,3},{6,0},{7,1},{8,14},{9,15},{10,... | collective-permute-start | bytes 36872 | tf_op jit(solution)/shard_map/ppermute | solution.py:379
  110.4 20.5 %collective-permute-start.19 = (bf16[8,768]{1,0:T(8,128)(2,1)S(1)}, bf16[8,768]{1,0:T(8,128)(2,1)S(1)}, u32[]{:S(2)}, u32[]{:S(2)}) collective-permute-start(bf16[8,768]{1,0:T(8,128)(2,1)S(1)} %fusion.8), channel_id=1, source_target_pairs={{0,4},{1,5},{2,6},{3,7},{4,0},{5,1},{6,2},{7,3},{8,12},{9,13},{10,... | collective-permute-start | bytes 36872 | tf_op jit(solution)/shard_map/ppermute | solution.py:379
  111.3 19.7 %collective-permute-start.18 = (bf16[8,768]{1,0:T(8,128)(2,1)S(1)}, bf16[8,768]{1,0:T(8,128)(2,1)S(1)}, u32[]{:S(2)}, u32[]{:S(2)}) collective-permute-start(bf16[8,768]{1,0:T(8,128)(2,1)S(1)} %fusion.8), channel_id=1, source_target_pairs={{0,2},{1,3},{2,0},{3,1},{4,6},{5,7},{6,4},{7,5},{8,10},{9,11},{10,... | collective-permute-start | bytes 36872 | tf_op jit(solution)/shard_map/ppermute | solution.py:379
  131.0 3.8 %collective-permute-start.21 = (bf16[8,768]{1,0:T(8,128)(2,1)S(1)}, bf16[8,768]{1,0:T(8,128)(2,1)S(1)}, u32[]{:S(2)}, u32[]{:S(2)}) collective-permute-start(bf16[8,768]{1,0:T(8,128)(2,1)S(1)} %maximum_maximum_fusion), channel_id=1, source_target_pairs={{0,8},{1,9},{2,10},{3,11},{4,12},{5,13},{6,14},{7,15},{8,0},{9,1},... | collective-permute-start | bytes 36872 | tf_op jit(solution)/shard_map/ppermute | solution.py:379
  (13 other events, 12.5 us)
